TPU v7x, 128 devices: a whole 4x4x4 slice. The times are simulated.
128 devices in a mesh: grp: 4 (over x_hi, core), dev: 32 (over z, y, x_lo).
Axes of the slice: x: 4 (x_hi: 2, x_lo: 2; x = x_hi * 2 + x_lo), y: 4, z: 4, core: 2. Of those that a mesh axis runs over, the one named last changes fastest.
Arguments:
- fields: float32 [24, 256, 128, 128], P(None, ('grp', 'dev')), may hold values from -6 to 6
- mix_matrix: float32 [24, 24], replicated, may hold values from -1.25 to 1.25
- laplace_matrix: float32 [24, 24], replicated, may hold values from -0.21875 to 0.21875
Outputs:
- rhs: float32 [24, 256, 128, 128], P(None, ('grp', 'dev'))
- weyl: float32 [2, 256, 128, 128], P(None, 'grp', 'dev')
All inputs are finite; a program needn't handle non-finite values.
Results may differ from a plain program's by a relative error of at most 0.0003.
Values sent between devices are 32-bit elements; how exact they have to be, the bound alone decides.
A program may use at most 192 MiB of HBM per device.

v0:
```python
import jax
import jax.numpy as jnp
from jax import lax
from jax.sharding import PartitionSpec as P


def with_halo(block, sides, width):
    for axis, dim in sides:
        count = lax.axis_size(axis)
        forward = [(i, i + 1) for i in range(count - 1)]
        forward.append((count - 1, 0))
        backward = [(target, source) for source, target in forward]
        low = lax.ppermute(
            lax.slice_in_dim(block, block.shape[dim] - width, None, axis=dim), axis, forward
        )
        high = lax.ppermute(lax.slice_in_dim(block, 0, width, axis=dim), axis, backward)
        block = jnp.concatenate([low, block, high], axis=dim)
    return block


def pad_periodic(field, dimension):
    length = field.shape[dimension]
    before = lax.slice_in_dim(field, length - 2, length, axis=dimension)
    after = lax.slice_in_dim(field, 0, 2, axis=dimension)
    return jnp.concatenate([before, field, after], axis=dimension)


def interior(padded, keep):
    result = padded
    for dimension in (1, 2, 3):
        if dimension != keep:
            result = lax.slice_in_dim(result, 2, result.shape[dimension] - 2, axis=dimension)
    return result


def stencil_values(padded, dimension):
    centre = interior(padded, dimension)
    length = centre.shape[dimension] - 4
    return [
        lax.slice_in_dim(centre, offset, offset + length, axis=dimension) for offset in range(5)
    ]


def first_diff(padded, dimension):
    values = stencil_values(padded, dimension)
    return (values[0] - 8.0 * values[1] + 8.0 * values[3] - values[4]) / 12.0


def second_diff(padded, dimension):
    values = stencil_values(padded, dimension)
    return (-values[0] + 16.0 * values[1] - 30.0 * values[2] + 16.0 * values[3] - values[4]) / 12.0


def laplacian(padded):
    return second_diff(padded, 1) + second_diff(padded, 2) + second_diff(padded, 3)


def evolution(padded, mix_matrix, laplace_matrix):
    centre = interior(padded, 0)
    laplace = laplacian(padded)
    result = jnp.einsum("fg,gzyx->fzyx", mix_matrix, centre, precision=lax.Precision.HIGHEST)
    result = result + jnp.einsum(
        "fg,gzyx->fzyx", laplace_matrix, laplace, precision=lax.Precision.HIGHEST
    )
    for dimension in (1, 2, 3):
        result = result + centre[11 + dimension][None] * first_diff(padded, dimension)
    return result


def contract(tensor, left, right):
    total = 0.0
    for first in range(3):
        for second in range(3):
            total = total + tensor[first][second] * left[first] * right[second]
    return total


def weyl_scalar(padded, zpos, ypos, xpos):
    table = ((0, 1, 2), (1, 3, 4), (2, 4, 5))
    metric = padded[0:6]
    curv_padded = padded[6:12]
    lap_metric = laplacian(metric)
    curvature = interior(curv_padded, 0)
    gradient = [first_diff(curv_padded, 3 - index) for index in range(3)]
    trace = curvature[0] + curvature[3] + curvature[5]
    electric = []
    curl = []
    for first in range(3):
        erow = []
        crow = []
        for second in range(3):
            value = (
                -0.5 * lap_metric[table[first][second]] - trace * curvature[table[first][second]]
            )
            for middle in range(3):
                value = value + curvature[table[first][middle]] * curvature[table[middle][second]]
            erow.append(value)
            next_one = (first + 1) % 3
            next_two = (first + 2) % 3
            crow.append(
                gradient[next_one][table[next_two][second]]
                - gradient[next_two][table[next_one][second]]
            )
        electric.append(erow)
        curl.append(crow)
    magnetic = [
        [0.5 * (curl[first][second] + curl[second][first]) for second in range(3)]
        for first in range(3)
    ]
    along_x = xpos[None, None, :]
    along_y = ypos[None, :, None]
    along_z = zpos[:, None, None]
    cylinder = jnp.sqrt(along_x * along_x + along_y * along_y)
    radius = jnp.sqrt(cylinder * cylinder + along_z * along_z)
    theta_vec = (
        along_z * along_x / (radius * cylinder),
        along_z * along_y / (radius * cylinder),
        -cylinder / radius,
    )
    phi_vec = (-along_y / cylinder, along_x / cylinder, 0.0)
    real_part = 0.5 * (
        contract(electric, theta_vec, theta_vec) - contract(electric, phi_vec, phi_vec)
    ) - contract(magnetic, theta_vec, phi_vec)
    imag_part = -contract(electric, theta_vec, phi_vec) - 0.5 * (
        contract(magnetic, theta_vec, theta_vec) - contract(magnetic, phi_vec, phi_vec)
    )
    return jnp.stack([real_part, imag_part])


def centred(index, count):
    return index.astype(jnp.float32) + 0.5 - 0.5 * count


def per_device(fields, mix_matrix, laplace_matrix):
    depth = fields.shape[1]
    rows = fields.shape[2]
    width = fields.shape[3]
    groups = lax.axis_size("grp")
    members = lax.axis_size("dev")
    total_depth = depth * groups * members
    slab = lax.axis_index("grp") * members + lax.axis_index("dev")
    zpadded = with_halo(fields, ((("grp", "dev"), 1),), 2)
    padded = pad_periodic(pad_periodic(zpadded, 2), 3)
    rhs = evolution(padded, mix_matrix, laplace_matrix)
    xpos = centred(jnp.arange(width, dtype=jnp.int32), width)
    zpos = centred(slab * depth + jnp.arange(depth, dtype=jnp.int32), total_depth)
    ypos = centred(jnp.arange(rows, dtype=jnp.int32), rows)
    local = weyl_scalar(padded[0:12], zpos, ypos, xpos)
    weyl = lax.all_to_all(local, "dev", split_axis=2, concat_axis=1, tiled=True)
    return (rhs, weyl)


def solution(mesh):
    return jax.shard_map(
        per_device,
        mesh=mesh,
        in_specs=(P(None, ("grp", "dev"), None, None), P(), P()),
        out_specs=(P(None, ("grp", "dev"), None, None), P(None, "grp", "dev", None)),
        check_vma=False,
    )
```

profile of v0, /device:TPU:96, one launch (start us, length us, event | category | flops | bytes accessed | tf_op | source)
XLA Modules:
  0.0 234.0 jit_solution(18402747833871870252)
XLA Ops:
  0.6 0.0 copy-start
  0.6 1.6 collective-permute-start
  2.2 3.5 %collective-permute-start.1 = (f32[24,2,128,128]{3,2,1,0:T(8,128)}, f32[24,2,128,128]{3,2,1,0:T(8,128)}, u32[]{:S(2)}, u32[]{:S(2)}) collective-permute-start(f32[24,2,128,128]{3,2,1,0:T(8,128)} %param.3), channel_id=1, source_target_pairs={{1,0},{2,1},{3,2},{4,3},{5,4},{6,5},{7,6},{8,7},{9,8},{10,9},{11,1... | collective-permute-start | bytes 9437192 | tf_op jit(solution)/shard_map/ppermute | solution.py:16
  5.8 0.1 broadcast_multiply_fusion
  5.8 2.0 add_add_fusion
  7.8 0.9 fusion.118
  8.7 0.0 copy-done
  8.7 7.7 %fusion.9 = f32[24,2,128,128]{3,0,2,1:T(8,128)} fusion(f32[24,2,128,128]{3,2,1,0:T(8,128)} %param.3, f32[24,24]{1,0:T(8,128)S(1)} %copy-done), kind=kOutput, calls=%fused_computation.35 | convolution fusion | flops 226492416 | bytes 6293760 | tf_op jit(solution)/shard_map/fg,gzyx->fzyx/dot_general | solution.py:61
  16.4 58.5 %collective-permute-done = f32[24,2,128,128]{3,2,1,0:T(8,128)S(1)} collective-permute-done((f32[24,2,128,128]{3,2,1,0:T(8,128)}, f32[24,2,128,128]{3,2,1,0:T(8,128)S(1)}, u32[]{:S(2)}, u32[]{:S(2)}) %collective-permute-start) | collective-permute-done | bytes 3145760 | tf_op jit(solution)/shard_map/ppermute | solution.py:13
  74.9 0.6 constant_dynamic-update-slice_fusion.6
  75.5 0.0 copy-done.4
  75.5 0.9 constant_dynamic-update-slice_fusion.5
  76.4 0.0 copy-start.8
  76.4 62.9 %collective-permute-done.1 = f32[24,2,128,128]{3,2,1,0:T(8,128)} collective-permute-done((f32[24,2,128,128]{3,2,1,0:T(8,128)}, f32[24,2,128,128]{3,2,1,0:T(8,128)}, u32[]{:S(2)}, u32[]{:S(2)}) %collective-permute-start.1) | collective-permute-done | bytes 3145760 | tf_op jit(solution)/shard_map/ppermute | solution.py:16
  139.3 2.6 %constant_dynamic-update-slice_fusion.4 = (f32[24,6,128,128]{3,2,1,0:T(8,128)S(1)}, f32[24,4,128,128]{3,2,1,0:T(8,128)S(1)}) fusion(f32[24,6,128,128]{3,2,1,0:T(8,128)S(1)} %get-tuple-element.31, f32[24,2,128,128]{3,2,1,0:T(8,128)} %collective-permute-done.1, f32[24,4,128,128]{3,2,1,0:T(8,128)S(1)} %get-tuple-element.32), kind=kLoop, calls=%fused_computation.203 | loop fusion | bytes 9437184 | tf_op jit(solution)/shard_map/concatenate | solution.py:17
  141.9 0.0 copy-done.8
  141.9 0.0 copy-start.7
  141.9 2.6 %copy-done.7 = f32[24,4,128,128]{3,2,1,0:T(8,128)} copy-done((f32[24,4,128,128]{3,2,1,0:T(8,128)}, f32[24,4,128,128]{3,2,1,0:T(8,128)S(1)}, u32[]{:S(2)}) %copy-start.7) | copy-done | bytes 6291480
  144.5 0.1 fusion.137
  144.6 5.7 %pad_maximum_fusion = f32[24,6,132,128]{3,2,1,0:T(8,128)} fusion(f32[24,6,2,128]{3,2,1,0:T(2,128)S(1)} %get-tuple-element.23, f32[24,6,128,128]{3,2,1,0:T(8,128)S(1)} %get-tuple-element.29, f32[24,6,2,128]{3,2,1,0:T(2,128)S(1)} %get-tuple-element.24), kind=kLoop, calls=%fused_computation.10 | loop fusion | flops 4866048 | bytes 19464192 | tf_op jit(solution)/shard_map/concatenate | solution.py:25
  150.3 14.3 %fusion.136 = (f32[24,6,132,2]{3,2,1,0:T(8,128)S(1)}, f32[24,6,132,2]{3,2,1,0:T(8,128)}) fusion(f32[24,6,132,128]{3,2,1,0:T(8,128)} %pad_maximum_fusion), kind=kLoop, calls=%fused_computation.214 | loop fusion | bytes 608256 | tf_op jit(solution)/shard_map/slice | solution.py:24
  164.5 0.0 slice-start.5
  164.6 4.4 %fusion.31 = f32[6,2,128,128]{3,2,1,0:T(8,128)S(1)} fusion(f32[24,6,132,2]{3,2,1,0:T(8,128)S(1)} %get-tuple-element.21, f32[24,6,2,128]{3,2,1,0:T(2,128)S(1)} %get-tuple-element.23, f32[24,6,128,128]{3,2,1,0:T(8,128)S(1)} %get-tuple-element.29, f32[24,6,2,128]{3,2,1,0:T(2,128)S(1)} %get-tuple-element.24, f32[24,6,132,2]{3,2,1,0:T(8,128)} %get-tuple-element.22), kind=kLoop, calls=%fused_computation.59 | loop fusion | flops 3538944 | bytes 10822656 | tf_op jit(solution)/shard_map/div | solution.py:46
  168.9 0.7 copy-done.3
  169.6 1.2 slice-done.3
  170.8 1.3 slice-done.4
  172.1 0.4 slice-done.5
  172.5 3.7 %fusion.46 = f32[6,2,128,128]{3,2,1,0:T(8,128)S(1)} fusion(f32[24,6,132,2]{3,2,1,0:T(8,128)S(1)} %get-tuple-element.21, f32[24,6,2,128]{3,2,1,0:T(2,128)S(1)} %get-tuple-element.23, f32[24,6,128,128]{3,2,1,0:T(8,128)S(1)} %get-tuple-element.29, f32[24,6,2,128]{3,2,1,0:T(2,128)S(1)} %get-tuple-element.24, f32[24,6,132,2]{3,2,1,0:T(8,128)S(1)} %bitcast.31, ...), kind=kLoop, calls=%fused_computation.93 | loop fusion | flops 8060928 | bytes 14754816 | tf_op jit(solution)/shard_map/add | solution.py:55
  176.3 0.0 copy-done.5
  176.3 0.0 copy-done.2
  176.3 0.0 copy-start.11
  176.3 0.0 copy-start.12
  176.3 0.0 copy-start.13
  176.3 0.0 copy-start.14
  176.3 0.0 copy-start.15
  176.4 0.0 copy-start.16
  176.4 2.3 fusion.35
  178.7 0.0 copy-start.17
  178.7 0.0 copy-start.18
  178.7 0.0 copy-done.11
  178.7 0.0 copy-done.12
  178.7 0.0 copy-done.13
  178.7 0.0 copy-done.14
  178.8 0.0 copy-done.15
  178.8 0.0 copy-done.16
  178.8 0.7 fusion.72
  179.5 0.0 copy-done.17
  179.5 0.0 copy-done.18
  179.6 0.5 fusion.82
  180.1 0.9 copy.42
  181.0 8.2 %all-to-all-start = ((f32[2,2,128,128]{3,0,1,2:T(2,128)}), f32[2,2,128,128]{3,0,1,2:T(2,128)}, u32[]{:S(2)}, u32[]{:S(2)}) async-start(f32[2,2,128,128]{3,0,1,2:T(2,128)} %copy.42), calls=%async_computation | async-start | bytes 524288 | tf_op jit(solution)/shard_map/all_to_all | solution.py:149
  189.2 0.0 copy-start.19
  189.2 0.0 slice-start.1
  189.2 0.0 slice-start.2
  189.2 25.8 %add_multiply_fusion = (f32[24,2,128,128]{3,2,1,0:T(8,128)}, f32[24,2,128,128]{3,2,1,0:T(8,128)}, f32[24,2,128,128]{3,2,1,0:T(8,128)}, f32[24,2,128,128]{3,2,1,0:T(8,128)}, f32[24,2,128,128]{3,2,1,0:T(8,128)}) fusion(f32[24,2,128,128]{3,2,1,0:T(8,128)} %collective-permute-done.1, f32[24,2,128,128]{3,2,1,0:T(8,128)} %param.3, ...), kind=kLoop, calls=%fused_computation.37 | loop fusion | flops 32243712 | bytes 41493504 | tf_op jit(solution)/shard_map/add | solution.py:55
  215.0 0.0 copy-done.19
  215.0 0.0 copy-start.6
  215.0 0.0 copy-start.9
  215.0 0.0 copy-start.10
  215.0 6.6 %fusion.7 = f32[2,128,128,24]{2,3,1,0:T(8,128)S(1)} fusion(f32[24,2,128,128]{3,2,1,0:T(8,128)} %get-tuple-element.16, f32[24,24]{1,0:T(8,128)S(1)} %copy-done.19), kind=kOutput, calls=%fused_computation.33 | convolution fusion | flops 226492416 | bytes 6293760 | tf_op jit(solution)/shard_map/fg,gzyx->fzyx/dot_general | solution.py:62
  221.7 0.0 copy-start.1
  221.7 10.6 %fusion.6 = f32[24,2,128,128]{3,2,1,0:T(8,128)} fusion(f32[24,2,128,128]{3,0,2,1:T(8,128)} %fusion.9, f32[2,128,128,24]{2,3,1,0:T(8,128)S(1)} %fusion.7, f32[24,2,128,128]{3,2,1,0:T(8,128)} %get-tuple-element.20, f32[24,2,128,128]{3,2,1,0:T(8,128)} %get-tuple-element.19, f32[24,2,128,128]{3,2,1,0:T(8,128)S(1)} %copy-done.9, ...), kind=kLoop, calls=%fused_computation.32 | loop fusion | flops 20447232 | bytes 44728320 | tf_op jit(solution)/shard_map/add | solution.py:66
  232.2 0.0 all-to-all-done
  232.3 1.7 copy.43
  (20 shorter events, 0.1 us)
Async XLA Ops:
  0.6 8.1 %copy-start = (f32[24,24]{1,0:T(8,128)S(1)}, f32[24,24]{1,0:T(8,128)}, u32[]{:S(2)}) copy-start(f32[24,24]{1,0:T(8,128)} %param.4) | copy-start | bytes 6916
  0.6 74.3 %collective-permute-start = (f32[24,2,128,128]{3,2,1,0:T(8,128)}, f32[24,2,128,128]{3,2,1,0:T(8,128)S(1)}, u32[]{:S(2)}, u32[]{:S(2)}) collective-permute-start(f32[24,2,128,128]{3,2,1,0:T(8,128)} %param.3), channel_id=1, source_target_pairs={{0,1},{1,2},{2,3},{3,4},{4,5},{5,6},{6,7},{7,8},{8,9},{9,10},{10,1... | collective-permute-start | bytes 9437192 | tf_op jit(solution)/shard_map/ppermute | solution.py:13
  2.2 137.1 %collective-permute-start.1 = (f32[24,2,128,128]{3,2,1,0:T(8,128)}, f32[24,2,128,128]{3,2,1,0:T(8,128)}, u32[]{:S(2)}, u32[]{:S(2)}) collective-permute-start(f32[24,2,128,128]{3,2,1,0:T(8,128)} %param.3), channel_id=1, source_target_pairs={{1,0},{2,1},{3,2},{4,3},{5,4},{6,5},{7,6},{8,7},{9,8},{10,9},{11,1... | collective-permute-start | bytes 9437192 | tf_op jit(solution)/shard_map/ppermute | solution.py:16
  16.4 59.0 %copy-start.4 = (f32[24,2,128,128]{3,2,1,0:T(8,128)S(1)}, f32[24,2,128,128]{3,2,1,0:T(8,128)}, u32[]{:S(2)}) copy-start(f32[24,2,128,128]{3,2,1,0:T(8,128)} %param.3) | copy-start | bytes 9437188
  74.9 101.4 %copy-start.5 = (f32[24,2,128,128]{3,2,1,0:T(8,128)}, f32[24,2,128,128]{3,2,1,0:T(8,128)S(1)}, u32[]{:S(2)}) copy-start(f32[24,2,128,128]{3,2,1,0:T(8,128)S(1)} %collective-permute-done) | copy-start | bytes 9437188
  76.4 65.5 %copy-start.8 = (f32[24,4,128,128]{3,2,1,0:T(8,128)}, f32[24,4,128,128]{3,2,1,0:T(8,128)S(1)}, u32[]{:S(2)}) copy-start(f32[24,4,128,128]{3,2,1,0:T(8,128)S(1)} %get-tuple-element.33) | copy-start | bytes 18874372
  141.9 2.6 %copy-start.7 = (f32[24,4,128,128]{3,2,1,0:T(8,128)}, f32[24,4,128,128]{3,2,1,0:T(8,128)S(1)}, u32[]{:S(2)}) copy-start(f32[24,4,128,128]{3,2,1,0:T(8,128)S(1)} %get-tuple-element.30) | copy-start | bytes 18874372
  144.5 31.8 %copy-start.2 = (f32[24,6,128,128]{3,2,1,0:T(8,128)}, f32[24,6,128,128]{3,2,1,0:T(8,128)S(1)}, u32[]{:S(2)}) copy-start(f32[24,6,128,128]{3,2,1,0:T(8,128)S(1)} %get-tuple-element.29) | copy-start | bytes 28311556
  164.5 5.1 %copy-start.3 = (f32[24,6,132,2]{3,2,1,0:T(8,128)}, f32[24,6,132,2]{3,2,1,0:T(8,128)S(1)}, u32[]{:S(2)}) copy-start(f32[24,6,132,2]{3,2,1,0:T(8,128)S(1)} %get-tuple-element.21) | copy-start | bytes 456196
  164.5 6.3 %slice-start.3 = ((s8[10027008]{0:T(1024)(128)(4,1)}), s8[4194304]{0:T(1024)(128)(4,1)S(1)}, s32[]{:S(2)}) async-start(s8[10027008]{0:T(1024)(128)(4,1)} %bitcast.30), calls=%async_computation.4 | async-start | bytes 8388608
  164.5 7.6 %slice-start.4 = ((s8[10027008]{0:T(1024)(128)(4,1)}), s8[4194304]{0:T(1024)(128)(4,1)S(1)}, s32[]{:S(2)}) async-start(s8[10027008]{0:T(1024)(128)(4,1)} %bitcast.30), calls=%async_computation.5 | async-start | bytes 8388608
  164.5 8.0 %slice-start.5 = ((s8[10027008]{0:T(1024)(128)(4,1)}), s8[1638400]{0:T(1024)(128)(4,1)S(1)}, s32[]{:S(2)}) async-start(s8[10027008]{0:T(1024)(128)(4,1)} %bitcast.30), calls=%async_computation.6 | async-start | bytes 3276800
  176.3 2.4 %copy-start.11 = (f32[128,128]{1,0:T(8,128)S(1)}, f32[128,128]{1,0:T(8,128)}, u32[]{:S(2)}) copy-start(f32[128,128]{1,0:T(8,128)} %get-tuple-element.42) | copy-start | bytes 196612
  176.3 2.4 %copy-start.12 = (f32[128,128]{1,0:T(8,128)S(1)}, f32[128,128]{1,0:T(8,128)}, u32[]{:S(2)}) copy-start(f32[128,128]{1,0:T(8,128)} %get-tuple-element.43) | copy-start | bytes 196612
  176.3 2.4 %copy-start.13 = (f32[128,128]{1,0:T(8,128)S(1)}, f32[128,128]{1,0:T(8,128)}, u32[]{:S(2)}) copy-start(f32[128,128]{1,0:T(8,128)} %get-tuple-element.44) | copy-start | bytes 196612
  176.3 2.4 %copy-start.14 = (f32[128,128]{1,0:T(8,128)S(1)}, f32[128,128]{1,0:T(8,128)}, u32[]{:S(2)}) copy-start(f32[128,128]{1,0:T(8,128)} %get-tuple-element.45) | copy-start | bytes 196612
  176.3 2.4 %copy-start.15 = (f32[128,128]{1,0:T(8,128)S(1)}, f32[128,128]{1,0:T(8,128)}, u32[]{:S(2)}) copy-start(f32[128,128]{1,0:T(8,128)} %get-tuple-element.47) | copy-start | bytes 196612
  176.4 2.4 %copy-start.16 = (f32[1,2,128,128]{3,2,1,0:T(8,128)S(1)}, f32[1,2,128,128]{3,2,1,0:T(8,128)}, u32[]{:S(2)}) copy-start(f32[1,2,128,128]{3,2,1,0:T(8,128)} %get-tuple-element.25) | copy-start | bytes 393220
  178.7 0.8 copy-start.17
  178.7 0.9 copy-start.18
  181.0 40.6 %slice-start = ((s8[9437184]{0:T(1024)(128)(4,1)}), s8[1048576]{0:T(1024)(128)(4,1)S(1)}, s32[]{:S(2)}) async-start(s8[9437184]{0:T(1024)(128)(4,1)} %bitcast.28), calls=%async_computation.1 | async-start | bytes 2097152
  181.0 51.3 %all-to-all-start = ((f32[2,2,128,128]{3,0,1,2:T(2,128)}), f32[2,2,128,128]{3,0,1,2:T(2,128)}, u32[]{:S(2)}, u32[]{:S(2)}) async-start(f32[2,2,128,128]{3,0,1,2:T(2,128)} %copy.42), calls=%async_computation | async-start | bytes 524288 | tf_op jit(solution)/shard_map/all_to_all | solution.py:149
  189.2 25.8 %copy-start.19 = (f32[24,24]{1,0:T(8,128)S(1)}, f32[24,24]{1,0:T(8,128)}, u32[]{:S(2)}) copy-start(f32[24,24]{1,0:T(8,128)} %param.5) | copy-start | bytes 6916
  189.2 32.4 %slice-start.1 = ((s8[9437184]{0:T(1024)(128)(4,1)}), s8[4194304]{0:T(1024)(128)(4,1)S(1)}, s32[]{:S(2)}) async-start(s8[9437184]{0:T(1024)(128)(4,1)} %bitcast.28), calls=%async_computation.2 | async-start | bytes 8388608
  189.2 32.4 %slice-start.2 = ((s8[9437184]{0:T(1024)(128)(4,1)}), s8[4194304]{0:T(1024)(128)(4,1)S(1)}, s32[]{:S(2)}) async-start(s8[9437184]{0:T(1024)(128)(4,1)} %bitcast.28), calls=%async_computation.3 | async-start | bytes 8388608
  215.0 6.6 %copy-start.6 = (f32[24,2,128,128]{3,2,1,0:T(8,128)S(1)}, f32[24,2,128,128]{3,2,1,0:T(8,128)}, u32[]{:S(2)}) copy-start(f32[24,2,128,128]{3,2,1,0:T(8,128)} %copy-done.5) | copy-start | bytes 9437188
  215.0 6.6 %copy-start.9 = (f32[24,2,128,128]{3,2,1,0:T(8,128)S(1)}, f32[24,2,128,128]{3,2,1,0:T(8,128)}, u32[]{:S(2)}) copy-start(f32[24,2,128,128]{3,2,1,0:T(8,128)} %get-tuple-element.17) | copy-start | bytes 9437188
  215.0 6.6 %copy-start.10 = (f32[24,2,128,128]{3,2,1,0:T(8,128)S(1)}, f32[24,2,128,128]{3,2,1,0:T(8,128)}, u32[]{:S(2)}) copy-start(f32[24,2,128,128]{3,2,1,0:T(8,128)} %get-tuple-element.18) | copy-start | bytes 9437188
  221.7 12.3 %copy-start.1 = (f32[24,24]{1,0:T(8,128)S(1)}, f32[24,24]{1,0:T(8,128)}, u32[]{:S(2)}) copy-start(f32[24,24]{1,0:T(8,128)} %param.4) | copy-start | bytes 6916
where the time goes:
time: 236 us; the launch traced here: 234 us
  waiting for transfers between devices  121 us (51%)
  other arithmetic  56.6 us (24%)
  local copies, waits for them, and re-layouts  27.4 us (12%)
  matrix products  14.3 us (6%)
  starting transfers between devices  13.3 us (6%)
    ppermute x1, waiting for transfers between devices, with_halo(): lax.ppermute(lax.slice_in_dim(block, 0, width, axis=dim), axis, backward)  62.9 us
    ppermute x1, waiting for transfers between devices, with_halo(): lax.ppermute(lax.slice_in_dim(block, block.shape[dim] - width, None, axis...  58.5 us
    add x2, other arithmetic, laplacian(): second_diff(padded, 1) + second_diff(padded, 2) + second_diff(padded, 3)  29.5 us
    slice x2, local copies, waits for them, and re-layouts, pad_periodic(): after = lax.slice_in_dim(field, 0, 2, axis=dimension)  14.4 us
    add x1, other arithmetic, evolution(): result + centre[11 + dimension][None] * first_diff(padded, dimension)  10.6 us
    all_to_all x1, starting transfers between devices, per_device(): weyl = lax.all_to_all(local, 'dev', split_axis=2, concat_axis=1, tiled=True)  8.18 us
    unnamed x54, local copies, waits for them, and re-layouts  7.89 us
    dot_general x1, matrix products, evolution(): jnp.einsum('fg,gzyx->fzyx', mix_matrix, centre, precision=lax.Precision.H...  7.73 us
  transfers between devices with their start and end apart: 3, of which 2 were waited for; matrix products, arithmetic and copies ran while one was open for 24% of the time, Pallas kernels for 0%

commit v1 on v0

v1 whole, which is shorter than its diff:
```python
import functools

import jax
import jax.numpy as jnp
from jax import lax
from jax.experimental import pallas as pl
from jax.experimental.pallas import tpu as pltpu
from jax.sharding import PartitionSpec as P

MESH = pl.DeviceIdType.MESH
F = 24
HALF = 12
ROWS = 8
LAG = 3
BLOCK = 12
COMPUTE = True
WEYL = True


def d12(m2, m1, p1, p2):
    return 8.0 * (p1 - m1) - (p2 - m2)


def kernel(groups, members, fields, mix, lapw, rhs, weyl, own, halo, tsum, w1, w2, wl,
           load_sem, send_p, recv_p, send_r, recv_r, send_d, wsend, wrecv, wlocal):
    depth = fields.shape[1]
    rows = fields.shape[2]
    width = fields.shape[3]
    tiles = rows // ROWS
    steps = 2 * tiles
    share = rows // members
    g = lax.axis_index("grp")
    d = lax.axis_index("dev")
    slabs = groups * members
    s = g * members + d
    odd = lax.rem(d, 2)
    partner = d + 1 - 2 * odd
    target = lax.rem(s + 2 - 4 * odd + slabs, slabs)
    target_id = {"grp": target // members, "dev": lax.rem(target, members)}
    nearby = lax.rem(s - 1 + 2 * odd + slabs, slabs)
    nearby_id = {"grp": nearby // members, "dev": lax.rem(nearby, members)}
    godd = lax.rem(g, 2)
    last = d >= members - 2
    first = d < 2
    cross = (last & (godd == 1)) | (first & (godd == 0))
    relays = jnp.logical_not(cross & ((d == members - 2) | (d == 1)))
    direct = cross & ((d == members - 1) | (d == 0))

    loads = []
    for half in range(2):
        part = pl.ds(half * HALF, HALF)
        loads.append(pltpu.make_async_copy(
            fields.at[part], own.at[part, :, pl.ds(8, rows), :], load_sem.at[half]))
    loads.append(pltpu.make_async_copy(
        fields.at[:, :, pl.ds(rows - 8, 8), :], own.at[:, :, pl.ds(0, 8), :], load_sem.at[2]))
    loads.append(pltpu.make_async_copy(
        fields.at[:, :, pl.ds(0, 8), :], own.at[:, :, pl.ds(rows + 8, 8), :], load_sem.at[3]))
    for load in loads:
        load.start()

    barrier = pltpu.get_barrier_semaphore()

    def greet(offset, _):
        pl.semaphore_signal(barrier, inc=1, device_id={"dev": lax.rem(d + offset, members)},
                            device_id_type=MESH)
        return 0

    lax.fori_loop(1, members, greet, 0)
    edge = jnp.where(last, 1, jnp.where(first, 1, 0))

    @pl.when(edge == 1)
    def _():
        other = lax.rem(g + jnp.where(last, 1, groups - 1), groups)
        base = jnp.where(last, 0, members - 2)
        for k in range(2):
            pl.semaphore_signal(barrier, inc=1, device_id={"grp": other, "dev": base + k},
                                device_id_type=MESH)

    pl.semaphore_wait(barrier, members - 1 + 2 * edge)

    def window(k):
        half = k // tiles
        tile = lax.rem(k, tiles)
        return half * HALF, tile * ROWS

    def own_chunk(k):
        f0, r0 = window(k)
        return own.at[pl.ds(f0, HALF), :, pl.ds(pl.multiple_of(r0 + 8, 8), ROWS), :]

    def halo_chunk(slot, k):
        f0, r0 = window(k)
        return halo.at[slot, pl.ds(f0, HALF), :, pl.ds(pl.multiple_of(r0, 8), ROWS), :]

    mine = 1 - odd

    def to_partner(k):
        return pltpu.make_async_remote_copy(
            own_chunk(k), halo_chunk(odd, k), send_p.at[k], recv_p.at[k],
            device_id={"dev": partner}, device_id_type=MESH)

    def from_partner(k):
        return pltpu.make_async_remote_copy(
            own_chunk(k), halo_chunk(mine, k), send_p.at[k], recv_p.at[k],
            device_id={"dev": partner}, device_id_type=MESH)

    def relay(k):
        return pltpu.make_async_remote_copy(
            halo_chunk(mine, k), halo_chunk(odd, k), send_r.at[k], recv_r.at[k],
            device_id=target_id, device_id_type=MESH)

    def straight(k):
        return pltpu.make_async_remote_copy(
            own_chunk(k), halo_chunk(mine, k), send_d.at[k], recv_r.at[k],
            device_id=nearby_id, device_id_type=MESH)

    def first_sends(k, _):
        to_partner(k).start()

        @pl.when(direct)
        def _():
            straight(k).start()
        return 0

    loads[0].wait()
    lax.fori_loop(0, tiles, first_sends, 0)
    loads[1].wait()
    lax.fori_loop(tiles, steps, first_sends, 0)
    loads[2].wait()
    loads[3].wait()

    if COMPUTE:
        def spread(at, _):
            c = at // F
            h = lax.rem(at, F)
            lap = lapw[c, h]
            w1[h, c] = jnp.full((8, 128), mix[c, h] - 7.5 * lap, jnp.float32)
            w2[h, c] = jnp.full((8, 128), lap * (1.0 / 12.0), jnp.float32)
            return 0

        lax.fori_loop(0, F * F, spread, 0)

    lane = lax.broadcasted_iota(jnp.int32, (ROWS, width), 1).astype(jnp.float32)
    line = lax.broadcasted_iota(jnp.int32, (ROWS, width), 0).astype(jnp.float32)

    def near(h, r0, p):
        def at(off):
            return own[h, p, pl.ds(r0 + 8 + off, ROWS), :]
        here = own[h, p, pl.ds(pl.multiple_of(r0 + 8, 8), ROWS), :]
        rows_at = pl.ds(pl.multiple_of(r0, 8), ROWS)
        xs = [pltpu.roll(here, 2, 1), pltpu.roll(here, 1, 1),
              pltpu.roll(here, width - 1, 1), pltpu.roll(here, width - 2, 1)]
        ys = [at(-2), at(-1), at(1), at(2)]
        if p == 0:
            zs = [halo[0, h, 0, rows_at, :], halo[0, h, 1, rows_at, :],
                  own[h, 1, pl.ds(pl.multiple_of(r0 + 8, 8), ROWS), :], halo[1, h, 0, rows_at, :]]
        else:
            zs = [halo[0, h, 1, rows_at, :],
                  own[h, 0, pl.ds(pl.multiple_of(r0 + 8, 8), ROWS), :],
                  halo[1, h, 0, rows_at, :], halo[1, h, 1, rows_at, :]]
        return here, xs, ys, zs

    def lap_sum(xs, ys, zs):
        one = (xs[1] + xs[2]) + (ys[1] + ys[2]) + (zs[1] + zs[2])
        two = (xs[0] + xs[3]) + (ys[0] + ys[3]) + (zs[0] + zs[3])
        return 16.0 * one - two

    def weyl_tile(tile):
        r0 = tile * ROWS
        xpos = lane + (0.5 - 0.5 * width)
        ypos = line + (r0.astype(jnp.float32) + (0.5 - 0.5 * rows))
        sq = xpos * xpos + ypos * ypos
        inv_s = lax.rsqrt(sq)
        cyl = sq * inv_s
        cosp = xpos * inv_s
        sinp = ypos * inv_s
        for p in range(depth):
            zpos = (s * depth + p).astype(jnp.float32) + (0.5 - 0.5 * slabs * depth)
            inv_r = lax.rsqrt(sq + zpos * zpos)
            zr = zpos * inv_r
            theta = (zr * cosp, zr * sinp, -(cyl * inv_r))
            phi = (-sinp, cosp)
            curv = []
            grad = []
            for h in range(6, 12):
                here, xs, ys, zs = near(h, r0, p)
                curv.append(here)
                grad.append((d12(*xs), d12(*ys), d12(*zs)))
            trace = curv[0] + curv[3] + curv[5]
            table = ((0, 1, 2), (1, 3, 4), (2, 4, 5))
            pairs = ((0, 0), (0, 1), (0, 2), (1, 1), (1, 2), (2, 2))

            def curl(i, j):
                n1, n2 = (i + 1) % 3, (i + 2) % 3
                return grad[table[n2][j]][n1] - grad[table[n1][j]][n2]

            real = None
            imag = None
            for at, (i, j) in enumerate(pairs):
                here, xs, ys, zs = near(at, r0, p)
                lap = lap_sum(xs, ys, zs) - 90.0 * here
                elec = lap * (-0.5 / 12.0) - trace * curv[at]
                for m in range(3):
                    elec = elec + curv[table[i][m]] * curv[table[m][j]]
                if i == j:
                    mag = curl(i, i) * (1.0 / 12.0)
                else:
                    mag = (curl(i, j) + curl(j, i)) * (0.5 / 12.0)
                fi = phi[i] if i < 2 else None
                fj = phi[j] if j < 2 else None
                tt = theta[i] * theta[j]
                both = tt if fi is None or fj is None else tt - fi * fj
                mixed = None
                for u, v in ((theta[i], fj), (theta[j], fi)):
                    if v is not None:
                        mixed = u * v if mixed is None else mixed + u * v
                if i == j:
                    both = 0.5 * both
                    mixed = None if mixed is None else 0.5 * mixed
                one = elec * both
                two = mag * both
                if mixed is not None:
                    one = one - mag * mixed
                    two = two + elec * mixed
                real = one if real is None else real + one
                imag = two if imag is None else imag + two
            imag = -imag
            per = ROWS // share
            for k in range(per):
                wl[tile * per + k, 0, p] = real[k * share:(k + 1) * share]
                wl[tile * per + k, 1, p] = imag[k * share:(k + 1) * share]

    def weyl_send(tile):
        per = ROWS // share
        for k in range(per):
            to = tile * per + k

            @pl.when(to == d)
            def _():
                pltpu.make_async_copy(
                    wl.at[to], weyl.at[:, pl.ds(d * depth, depth)], wlocal).start()

            @pl.when(to != d)
            def _():
                pltpu.make_async_remote_copy(
                    wl.at[to], weyl.at[:, pl.ds(d * depth, depth)], wsend, wrecv,
                    device_id={"dev": to}, device_id_type=MESH).start()

    def rhs_tile(tile):
        r0 = tile * ROWS
        mid = pl.ds(pl.multiple_of(r0 + 8, 8), ROWS)
        out = pl.ds(pl.multiple_of(r0, 8), ROWS)

        def stencil(h4, _):
            for p in range(depth):
                bz = own[12, p, mid, :] * (1.0 / 12.0)
                by = own[13, p, mid, :] * (1.0 / 12.0)
                bx = own[14, p, mid, :] * (1.0 / 12.0)
                for k in range(4):
                    h = h4 * 4 + k
                    here, xs, ys, zs = near(h, r0, p)
                    tsum[h, p] = lap_sum(xs, ys, zs)
                    rhs[h, p, out, :] = bx * d12(*xs) + by * d12(*ys) + bz * d12(*zs)
            return 0

        lax.fori_loop(0, F // 4, stencil, 0)
        for c0 in range(0, F, BLOCK):
            def mixing(h4, acc):
                for k in range(4):
                    h = h4 * 4 + k
                    acc = acc + w1[h, pl.ds(c0, BLOCK)][:, None] * own[h, :, mid, :][None]
                    acc = acc + w2[h, pl.ds(c0, BLOCK)][:, None] * tsum[h][None]
                return acc
            start = rhs[pl.ds(c0, BLOCK), :, out, :]
            rhs[pl.ds(c0, BLOCK), :, out, :] = lax.fori_loop(0, F // 4, mixing, start)

    def step(k, _):
        @pl.when(k < steps)
        def _():
            from_partner(k).wait_recv()

            @pl.when(relays)
            def _():
                relay(k).start()

        j = k - LAG

        @pl.when(j >= 0)
        def _():
            pltpu.make_async_remote_copy(
                own_chunk(j), halo_chunk(odd, j), send_r.at[j], recv_r.at[j],
                device_id={"dev": partner}, device_id_type=MESH).wait_recv()
            if WEYL:
                @pl.when((j >= 1) & (j <= tiles))
                def _():
                    weyl_send(j - 1)

            if COMPUTE:
                @pl.when(j < tiles)
                def _():
                    weyl_tile(j)

                @pl.when(j >= tiles)
                def _():
                    rhs_tile(j - tiles)
        return 0

    lax.fori_loop(0, steps + LAG, step, 0)

    def finish(k, _):
        to_partner(k).wait_send()

        @pl.when(relays)
        def _():
            relay(k).wait_send()

        @pl.when(direct)
        def _():
            straight(k).wait_send()
        return 0

    lax.fori_loop(0, steps, finish, 0)
    if WEYL:
        sent = wl.at[pl.ds(0, members - 1)]
        pltpu.make_async_copy(sent, sent, wsend).wait()
        came = weyl.at[:, pl.ds(0, depth * (members - 1))]
        pltpu.make_async_copy(came, came, wrecv).wait()
        pltpu.make_async_copy(wl.at[0], weyl.at[:, pl.ds(0, depth)], wlocal).wait()


def per_device(groups, members, fields, mix_matrix, laplace_matrix):
    depth, rows, width = fields.shape[1:]
    share = rows // members
    steps = 2 * (rows // ROWS)
    dma = pltpu.SemaphoreType.DMA
    return pl.pallas_call(
        functools.partial(kernel, groups, members),
        out_shape=(
            jax.ShapeDtypeStruct(fields.shape, jnp.float32),
            jax.ShapeDtypeStruct((2, depth * members, share, width), jnp.float32),
        ),
        in_specs=[
            pl.BlockSpec(memory_space=pltpu.HBM),
            pl.BlockSpec(memory_space=pltpu.SMEM),
            pl.BlockSpec(memory_space=pltpu.SMEM),
        ],
        out_specs=(pl.BlockSpec(memory_space=pltpu.VMEM), pl.BlockSpec(memory_space=pl.ANY)),
        scratch_shapes=[
            pltpu.VMEM((F, depth, rows + 16, width), jnp.float32),
            pltpu.VMEM((2, F, depth, rows, width), jnp.float32),
            pltpu.VMEM((F, depth, ROWS, width), jnp.float32),
            pltpu.VMEM((F, F, 8, 128), jnp.float32),
            pltpu.VMEM((F, F, 8, 128), jnp.float32),
            pltpu.VMEM((members, 2, depth, share, width), jnp.float32),
            dma((4,)), dma((steps,)), dma((steps,)), dma((steps,)), dma((steps,)), dma((steps,)),
            dma, dma, dma,
        ],
        compiler_params=pltpu.CompilerParams(
            collective_id=0, has_side_effects=True, vmem_limit_bytes=40 * 1024 * 1024
        ),
    )(fields, mix_matrix, laplace_matrix)


def solution(mesh):
    groups, members = mesh.shape["grp"], mesh.shape["dev"]
    return jax.shard_map(
        functools.partial(per_device, groups, members),
        mesh=mesh,
        in_specs=(P(None, ("grp", "dev"), None, None), P(), P()),
        out_specs=(P(None, ("grp", "dev"), None, None), P(None, "grp", "dev", None)),
        check_vma=False,
    )
```

time: 236 us -> 113 us (0.48)
  the two profiles are of different devices: /device:TPU:96 before, /device:TPU:9 now
where the time goes in v1:
time: 113 us; the launch traced here: 112 us
  Pallas kernels  106 us (94%)
  local copies, waits for them, and re-layouts  5.66 us (5%)
    pallas_call x1, Pallas kernels, per_device(): pl.pallas_call(functools.partial(kernel, groups, members), out_shape=(jax...  106 us
    unnamed x8, local copies, waits for them, and re-layouts  5.66 us

profile of v1, /device:TPU:9, one launch (start us, length us, event | category | flops | bytes accessed | tf_op | source)
XLA Modules:
  0.0 112.4 jit_solution(15272408700526419849)
XLA Ops:
  0.6 0.0 copy-start
  0.6 1.9 %copy-done = f32[24,2,128,128]{3,2,1,0:T(8,128)S(1)} copy-done((f32[24,2,128,128]{3,2,1,0:T(8,128)S(1)}, f32[24,2,128,128]{3,2,1,0:T(8,128)}, u32[]{:S(2)}) %copy-start) | copy-done | bytes 3145752
  2.5 0.0 copy-start.1
  2.5 0.7 copy-done.1
  3.2 0.0 copy-start.2
  3.2 0.7 copy-done.2
  3.9 106.1 %shard_map.50 = (f32[24,2,128,128]{3,2,1,0:T(8,128)S(1)}, f32[2,64,4,128]{3,2,1,0:T(4,128)S(1)}) custom-call(f32[24,2,128,128]{3,2,1,0:T(8,128)S(1)} %copy-done, f32[24,24]{1,0:T(8,128)S(1)} %copy-done.1, f32[24,24]{1,0:T(8,128)S(1)} %copy-done.2), custom_call_target="tpu_custom_call" | custom-call | tf_op jit(solution)/shard_map/pallas_call | solution.py:335
  110.1 1.7 %copy.7 = f32[24,2,128,128]{3,2,1,0:T(8,128)} copy(f32[24,2,128,128]{3,2,1,0:T(8,128)S(1)} %get-tuple-element.4) | data formatting | bytes 6291456
  111.7 0.7 copy.8
Async XLA Ops:
  0.6 1.9 %copy-start = (f32[24,2,128,128]{3,2,1,0:T(8,128)S(1)}, f32[24,2,128,128]{3,2,1,0:T(8,128)}, u32[]{:S(2)}) copy-start(f32[24,2,128,128]{3,2,1,0:T(8,128)} %fields.1) | copy-start | bytes 9437188
  2.5 0.7 copy-start.1
  3.2 0.7 copy-start.2

commit v2 on v1

--- a/solution.py
+++ b/solution.py
@@ -11,7 +11,8 @@
 F = 24
 HALF = 12
 ROWS = 8
-LAG = 3
+LAG = 8
+SUB = 1
 BLOCK = 12
 COMPUTE = True
 WEYL = True
@@ -21,13 +22,14 @@
     return 8.0 * (p1 - m1) - (p2 - m2)
 
 
-def kernel(groups, members, fields, mix, lapw, rhs, weyl, own, halo, tsum, w1, w2, wl,
-           load_sem, send_p, recv_p, send_r, recv_r, send_d, wsend, wrecv, wlocal):
+def kernel(groups, members, fields, mix_in, lap_in, rhs, weyl, own, halo, tsum, w1, w2, wl,
+           mix, lapw, wrow, load_sem, send_p, recv_p, send_r, recv_r, send_d, wsend, wrecv, wlocal):
     depth = fields.shape[1]
     rows = fields.shape[2]
     width = fields.shape[3]
     tiles = rows // ROWS
     steps = 2 * tiles
+    width_f = HALF // SUB
     share = rows // members
     g = lax.axis_index("grp")
     d = lax.axis_index("dev")
@@ -55,6 +57,8 @@
         fields.at[:, :, pl.ds(rows - 8, 8), :], own.at[:, :, pl.ds(0, 8), :], load_sem.at[2]))
     loads.append(pltpu.make_async_copy(
         fields.at[:, :, pl.ds(0, 8), :], own.at[:, :, pl.ds(rows + 8, 8), :], load_sem.at[3]))
+    loads.append(pltpu.make_async_copy(mix_in, mix, load_sem.at[4]))
+    loads.append(pltpu.make_async_copy(lap_in, lapw, load_sem.at[5]))
     for load in loads:
         load.start()
 
@@ -79,17 +83,16 @@
     pl.semaphore_wait(barrier, members - 1 + 2 * edge)
 
     def window(k):
-        half = k // tiles
-        tile = lax.rem(k, tiles)
-        return half * HALF, tile * ROWS
+        part, sub = k // SUB, lax.rem(k, SUB)
+        return (part // tiles) * HALF + sub * width_f, lax.rem(part, tiles) * ROWS
 
     def own_chunk(k):
         f0, r0 = window(k)
-        return own.at[pl.ds(f0, HALF), :, pl.ds(pl.multiple_of(r0 + 8, 8), ROWS), :]
+        return own.at[pl.ds(f0, width_f), :, pl.ds(pl.multiple_of(r0 + 8, 8), ROWS), :]
 
     def halo_chunk(slot, k):
         f0, r0 = window(k)
-        return halo.at[slot, pl.ds(f0, HALF), :, pl.ds(pl.multiple_of(r0, 8), ROWS), :]
+        return halo.at[slot, pl.ds(f0, width_f), :, pl.ds(pl.multiple_of(r0, 8), ROWS), :]
 
     mine = 1 - odd
 
@@ -115,47 +118,51 @@
 
     def first_sends(k, _):
         to_partner(k).start()
-
-        @pl.when(direct)
-        def _():
-            straight(k).start()
         return 0
 
     loads[0].wait()
-    lax.fori_loop(0, tiles, first_sends, 0)
+    lax.fori_loop(0, tiles * SUB, first_sends, 0)
     loads[1].wait()
-    lax.fori_loop(tiles, steps, first_sends, 0)
+    lax.fori_loop(tiles * SUB, steps * SUB, first_sends, 0)
     loads[2].wait()
     loads[3].wait()
 
+    loads[4].wait()
+    loads[5].wait()
     if COMPUTE:
-        def spread(at, _):
-            c = at // F
-            h = lax.rem(at, F)
-            lap = lapw[c, h]
-            w1[h, c] = jnp.full((8, 128), mix[c, h] - 7.5 * lap, jnp.float32)
-            w2[h, c] = jnp.full((8, 128), lap * (1.0 / 12.0), jnp.float32)
+        lap_all = lapw[...]
+        for at, table in enumerate((mix[...] - 7.5 * lap_all, lap_all * (1.0 / 12.0))):
+            for h in range(F):
+                wrow[at, h] = jnp.broadcast_to(table[:, h:h + 1], (F, 128))
+
+        def spread(h, _):
+            for at, into in enumerate((w1, w2)):
+                for c in range(F):
+                    into[h, c] = jnp.broadcast_to(wrow[at, h, c:c + 1, :], (8, 128))
             return 0
 
-        lax.fori_loop(0, F * F, spread, 0)
+        lax.fori_loop(0, F, spread, 0)
 
     lane = lax.broadcasted_iota(jnp.int32, (ROWS, width), 1).astype(jnp.float32)
     line = lax.broadcasted_iota(jnp.int32, (ROWS, width), 0).astype(jnp.float32)
 
-    def near(h, r0, p):
+    def near(h, r0, p, halos=True):
         def at(off):
             return own[h, p, pl.ds(r0 + 8 + off, ROWS), :]
-        here = own[h, p, pl.ds(pl.multiple_of(r0 + 8, 8), ROWS), :]
+        mid = pl.ds(pl.multiple_of(r0 + 8, 8), ROWS)
+        here = own[h, p, mid, :]
         rows_at = pl.ds(pl.multiple_of(r0, 8), ROWS)
         xs = [pltpu.roll(here, 2, 1), pltpu.roll(here, 1, 1),
               pltpu.roll(here, width - 1, 1), pltpu.roll(here, width - 2, 1)]
         ys = [at(-2), at(-1), at(1), at(2)]
+        other = own[h, 1 - p, mid, :]
+        if not halos:
+            return here, xs, ys, other
         if p == 0:
             zs = [halo[0, h, 0, rows_at, :], halo[0, h, 1, rows_at, :],
-                  own[h, 1, pl.ds(pl.multiple_of(r0 + 8, 8), ROWS), :], halo[1, h, 0, rows_at, :]]
+                  other, halo[1, h, 0, rows_at, :]]
         else:
-            zs = [halo[0, h, 1, rows_at, :],
-                  own[h, 0, pl.ds(pl.multiple_of(r0 + 8, 8), ROWS), :],
+            zs = [halo[0, h, 1, rows_at, :], other,
                   halo[1, h, 0, rows_at, :], halo[1, h, 1, rows_at, :]]
         return here, xs, ys, zs
 
@@ -245,50 +252,102 @@
                     wl.at[to], weyl.at[:, pl.ds(d * depth, depth)], wsend, wrecv,
                     device_id={"dev": to}, device_id_type=MESH).start()
 
-    def rhs_tile(tile):
+    def mixed(tile, h0, h1, with_own):
+        mid = pl.ds(pl.multiple_of(tile * ROWS + 8, 8), ROWS)
+        out = pl.ds(pl.multiple_of(tile * ROWS, 8), ROWS)
+        for c0 in range(0, F, BLOCK):
+            def mixing(h4, acc):
+                for k in range(4):
+                    h = h4 * 4 + k
+                    if with_own:
+                        acc = acc + w1[h, pl.ds(c0, BLOCK)][:, None] * own[h, :, mid, :][None]
+                    acc = acc + w2[h, pl.ds(c0, BLOCK)][:, None] * tsum[h][None]
+                return acc
+            start = rhs[pl.ds(c0, BLOCK), :, out, :]
+            rhs[pl.ds(c0, BLOCK), :, out, :] = lax.fori_loop(h0 // 4, h1 // 4, mixing, start)
+
+    def rhs_early(tile):
         r0 = tile * ROWS
         mid = pl.ds(pl.multiple_of(r0 + 8, 8), ROWS)
         out = pl.ds(pl.multiple_of(r0, 8), ROWS)
 
-        def stencil(h4, _):
+        def stencil(halos, h4, _):
             for p in range(depth):
                 bz = own[12, p, mid, :] * (1.0 / 12.0)
                 by = own[13, p, mid, :] * (1.0 / 12.0)
                 bx = own[14, p, mid, :] * (1.0 / 12.0)
                 for k in range(4):
                     h = h4 * 4 + k
-                    here, xs, ys, zs = near(h, r0, p)
-                    tsum[h, p] = lap_sum(xs, ys, zs)
-                    rhs[h, p, out, :] = bx * d12(*xs) + by * d12(*ys) + bz * d12(*zs)
+                    here, xs, ys, zs = near(h, r0, p, halos)
+                    if halos:
+                        tsum[h, p] = lap_sum(xs, ys, zs)
+                        dz = d12(*zs)
+                    else:
+                        one = (xs[1] + xs[2]) + (ys[1] + ys[2]) + zs
+                        two = (xs[0] + xs[3]) + (ys[0] + ys[3])
+                        tsum[h, p] = 16.0 * one - two
+                        dz = (8.0 if p == 0 else -8.0) * zs
+                    rhs[h, p, out, :] = bx * d12(*xs) + by * d12(*ys) + bz * dz
             return 0
 
-        lax.fori_loop(0, F // 4, stencil, 0)
-        for c0 in range(0, F, BLOCK):
-            def mixing(h4, acc):
+        lax.fori_loop(0, HALF // 4, functools.partial(stencil, True), 0)
+        lax.fori_loop(HALF // 4, F // 4, functools.partial(stencil, False), 0)
+        mixed(tile, 0, F, True)
+
+    def rhs_late(tile):
+        r0 = tile * ROWS
+        mid = pl.ds(pl.multiple_of(r0 + 8, 8), ROWS)
+        out = pl.ds(pl.multiple_of(r0, 8), ROWS)
+
+        def planes(h4, _):
+            for p in range(depth):
+                bz = own[12, p, mid, :] * (1.0 / 12.0)
                 for k in range(4):
                     h = h4 * 4 + k
-                    acc = acc + w1[h, pl.ds(c0, BLOCK)][:, None] * own[h, :, mid, :][None]
-                    acc = acc + w2[h, pl.ds(c0, BLOCK)][:, None] * tsum[h][None]
-                return acc
-            start = rhs[pl.ds(c0, BLOCK), :, out, :]
-            rhs[pl.ds(c0, BLOCK), :, out, :] = lax.fori_loop(0, F // 4, mixing, start)
-
-    def step(k, _):
-        @pl.when(k < steps)
-        def _():
-            from_partner(k).wait_recv()
-
-            @pl.when(relays)
-            def _():
-                relay(k).start()
-
-        j = k - LAG
+                    below = halo[0, h, 1, out, :]
+                    above = halo[1, h, 0, out, :]
+                    if p == 0:
+                        far = halo[0, h, 0, out, :]
+                        tsum[h, p] = 16.0 * below - (far + above)
+                        dz = (far - above) - 8.0 * below
+                    else:
+                        far = halo[1, h, 1, out, :]
+                        tsum[h, p] = 16.0 * above - (below + far)
+                        dz = 8.0 * above + (below - far)
+                    rhs[h, p, out, :] = rhs[h, p, out, :] + bz * dz
+            return 0
+
+        lax.fori_loop(HALF // 4, F // 4, planes, 0)
+        mixed(tile, HALF, F, False)
+
+    def relay_step(k, _):
+        from_partner(k).wait_recv()
+
+        @pl.when(relays)
+        def _():
+            relay(k).start()
+
+        @pl.when(direct)
+        def _():
+            straight(k).start()
+        return 0
+
+    def relayed(k, _):
+        pltpu.make_async_remote_copy(
+            own_chunk(k), halo_chunk(odd, k), send_r.at[k], recv_r.at[k],
+            device_id={"dev": partner}, device_id_type=MESH).wait_recv()
+        return 0
+
+    def step(part, _):
+        @pl.when(part < steps)
+        def _():
+            lax.fori_loop(part * SUB, part * SUB + SUB, relay_step, 0)
+
+        j = part - LAG
 
         @pl.when(j >= 0)
         def _():
-            pltpu.make_async_remote_copy(
-                own_chunk(j), halo_chunk(odd, j), send_r.at[j], recv_r.at[j],
-                device_id={"dev": partner}, device_id_type=MESH).wait_recv()
+            lax.fori_loop(j * SUB, j * SUB + SUB, relayed, 0)
             if WEYL:
                 @pl.when((j >= 1) & (j <= tiles))
                 def _():
@@ -298,10 +357,11 @@
                 @pl.when(j < tiles)
                 def _():
                     weyl_tile(j)
+                    rhs_early(j)
 
                 @pl.when(j >= tiles)
                 def _():
-                    rhs_tile(j - tiles)
+                    rhs_late(j - tiles)
         return 0
 
     lax.fori_loop(0, steps + LAG, step, 0)
@@ -318,7 +378,7 @@
             straight(k).wait_send()
         return 0
 
-    lax.fori_loop(0, steps, finish, 0)
+    lax.fori_loop(0, steps * SUB, finish, 0)
     if WEYL:
         sent = wl.at[pl.ds(0, members - 1)]
         pltpu.make_async_copy(sent, sent, wsend).wait()
@@ -330,7 +390,9 @@
 def per_device(groups, members, fields, mix_matrix, laplace_matrix):
     depth, rows, width = fields.shape[1:]
     share = rows // members
-    steps = 2 * (rows // ROWS)
+    chunks = 2 * (rows // ROWS) * SUB
+    arrays = [pltpu.with_memory_space_constraint(a, pltpu.HBM)
+              for a in (fields, mix_matrix, laplace_matrix)]
     dma = pltpu.SemaphoreType.DMA
     return pl.pallas_call(
         functools.partial(kernel, groups, members),
@@ -340,8 +402,8 @@
         ),
         in_specs=[
             pl.BlockSpec(memory_space=pltpu.HBM),
-            pl.BlockSpec(memory_space=pltpu.SMEM),
-            pl.BlockSpec(memory_space=pltpu.SMEM),
+            pl.BlockSpec(memory_space=pltpu.HBM),
+            pl.BlockSpec(memory_space=pltpu.HBM),
         ],
         out_specs=(pl.BlockSpec(memory_space=pltpu.VMEM), pl.BlockSpec(memory_space=pl.ANY)),
         scratch_shapes=[
@@ -351,13 +413,16 @@
             pltpu.VMEM((F, F, 8, 128), jnp.float32),
             pltpu.VMEM((F, F, 8, 128), jnp.float32),
             pltpu.VMEM((members, 2, depth, share, width), jnp.float32),
-            dma((4,)), dma((steps,)), dma((steps,)), dma((steps,)), dma((steps,)), dma((steps,)),
+            pltpu.VMEM((F, F), jnp.float32),
+            pltpu.VMEM((F, F), jnp.float32),
+            pltpu.VMEM((2, F, F, 128), jnp.float32),
+            dma((6,)), dma((chunks,)), dma((chunks,)), dma((chunks,)), dma((chunks,)), dma((chunks,)),
             dma, dma, dma,
         ],
         compiler_params=pltpu.CompilerParams(
             collective_id=0, has_side_effects=True, vmem_limit_bytes=40 * 1024 * 1024
         ),
-    )(fields, mix_matrix, laplace_matrix)
+    )(*arrays)
 
 
 def solution(mesh):

time: 113 us -> 91.1 us (0.81)
  the two profiles are of different devices: /device:TPU:9 before, /device:TPU:1 now
where the time goes in v2:
time: 91.1 us; the launch traced here: 91 us
  Pallas kernels  88 us (97%)
  local copies, waits for them, and re-layouts  2.37 us (3%)
    pallas_call x1, Pallas kernels, per_device(): pl.pallas_call(functools.partial(kernel, groups, members), out_shape=(jax...  88 us
    unnamed x2, local copies, waits for them, and re-layouts  2.37 us

profile of v2, /device:TPU:1, one launch (start us, length us, event | category | flops | bytes accessed | tf_op | source)
XLA Modules:
  0.0 91.0 jit_solution(12542350833163900408)
XLA Ops:
  0.6 88.0 %shard_map.50 = (f32[24,2,128,128]{3,2,1,0:T(8,128)S(1)}, f32[2,64,4,128]{3,2,1,0:T(4,128)S(1)}) custom-call(f32[24,2,128,128]{3,2,1,0:T(8,128)} %fields.1, f32[24,24]{1,0:T(8,128)} %mix_in.1, f32[24,24]{1,0:T(8,128)} %lap_in.1), custom_call_target="tpu_custom_call" | custom-call | tf_op jit(solution)/shard_map/pallas_call | solution.py:397
  88.7 1.7 %copy.7 = f32[24,2,128,128]{3,2,1,0:T(8,128)} copy(f32[24,2,128,128]{3,2,1,0:T(8,128)S(1)} %get-tuple-element.4) | data formatting | bytes 6291456
  90.3 0.7 copy.8

commit v3 on v2

--- a/solution.py
+++ b/solution.py
@@ -12,7 +12,11 @@
 HALF = 12
 ROWS = 8
 LAG = 8
-SUB = 1
+TAIL = 4
+HOLD_P = 3
+HOLD_R = 2
+HOLD_D = 4
+HOLD_V = 5
 BLOCK = 12
 COMPUTE = True
 WEYL = True
@@ -22,14 +26,14 @@
     return 8.0 * (p1 - m1) - (p2 - m2)
 
 
-def kernel(groups, members, fields, mix_in, lap_in, rhs, weyl, own, halo, tsum, w1, w2, wl,
-           mix, lapw, wrow, load_sem, send_p, recv_p, send_r, recv_r, send_d, wsend, wrecv, wlocal):
+def kernel(groups, members, fields, mix_in, lap_in, rhs, weyl, own, halo, via, tsum, w1, w2, wl,
+           mix, lapw, wrow, load_sem, send_p, recv_p, send_r, recv_r, send_d, recv_d, wsend, wrecv, wlocal,
+           up, far, ready):
     depth = fields.shape[1]
     rows = fields.shape[2]
     width = fields.shape[3]
     tiles = rows // ROWS
     steps = 2 * tiles
-    width_f = HALF // SUB
     share = rows // members
     g = lax.axis_index("grp")
     d = lax.axis_index("dev")
@@ -39,14 +43,17 @@
     partner = d + 1 - 2 * odd
     target = lax.rem(s + 2 - 4 * odd + slabs, slabs)
     target_id = {"grp": target // members, "dev": lax.rem(target, members)}
-    nearby = lax.rem(s - 1 + 2 * odd + slabs, slabs)
-    nearby_id = {"grp": nearby // members, "dev": lax.rem(nearby, members)}
+    end = members - 1
     godd = lax.rem(g, 2)
-    last = d >= members - 2
-    first = d < 2
-    cross = (last & (godd == 1)) | (first & (godd == 0))
-    relays = jnp.logical_not(cross & ((d == members - 2) | (d == 1)))
-    direct = cross & ((d == members - 1) | (d == 0))
+
+    def group(by):
+        return {"grp": lax.rem(g + by + groups, groups)}
+
+    hub = ((godd == 1) & (d == end - 1)) | ((godd == 0) & (d == 1))
+    direct = ((godd == 1) & (d == end)) | ((godd == 0) & (d == 0))
+    relays = jnp.logical_not(hub)
+    hub_id = {"grp": lax.rem(g + 1 - 2 * godd + groups, groups), "dev": jnp.where(d == 0, end - 1, 1)}
+    hub_target = {**group(2), "dev": jnp.where(d == 1, 0, end)}
 
     loads = []
     for half in range(2):
@@ -64,66 +71,142 @@
 
     barrier = pltpu.get_barrier_semaphore()
 
-    def greet(offset, _):
-        pl.semaphore_signal(barrier, inc=1, device_id={"dev": lax.rem(d + offset, members)},
-                            device_id_type=MESH)
+    def hello(to):
+        pl.semaphore_signal(barrier, inc=1, device_id=to, device_id_type=MESH)
+
+    def greet(to, _):
+        hello({"dev": to})
         return 0
 
-    lax.fori_loop(1, members, greet, 0)
-    edge = jnp.where(last, 1, jnp.where(first, 1, 0))
-
-    @pl.when(edge == 1)
-    def _():
-        other = lax.rem(g + jnp.where(last, 1, groups - 1), groups)
-        base = jnp.where(last, 0, members - 2)
-        for k in range(2):
-            pl.semaphore_signal(barrier, inc=1, device_id={"grp": other, "dev": base + k},
-                                device_id_type=MESH)
-
-    pl.semaphore_wait(barrier, members - 1 + 2 * edge)
-
-    def window(k):
-        part, sub = k // SUB, lax.rem(k, SUB)
-        return (part // tiles) * HALF + sub * width_f, lax.rem(part, tiles) * ROWS
-
-    def own_chunk(k):
-        f0, r0 = window(k)
-        return own.at[pl.ds(f0, width_f), :, pl.ds(pl.multiple_of(r0 + 8, 8), ROWS), :]
-
-    def halo_chunk(slot, k):
-        f0, r0 = window(k)
-        return halo.at[slot, pl.ds(f0, width_f), :, pl.ds(pl.multiple_of(r0, 8), ROWS), :]
+    @pl.when(odd == 1)
+    def _():
+        hello({"dev": d - 1})
+
+    lax.fori_loop(d + 1, members, greet, 0)
+
+    @pl.when((d == 0) & (godd == 1))
+    def _():
+        hello({**group(-1), "dev": end - 1})
+
+    @pl.when((d == 1) & (godd == 1))
+    def _():
+        hello({**group(-1), "dev": end})
+
+    @pl.when((d == 0) & (godd == 0))
+    def _():
+        hello({**group(1), "dev": end - 1})
+        hello({**group(2), "dev": 1})
+
+    @pl.when((d == 1) & (godd == 0))
+    def _():
+        hello({**group(1), "dev": end})
+
+    @pl.when((d == end) & (godd == 1))
+    def _():
+        hello({**group(2), "dev": end - 1})
+
+    extra = jnp.where(d == end, 1, jnp.where(d == end - 1, 1 + godd, jnp.where(d == 1, 1 - godd, 0)))
+    pl.semaphore_wait(barrier, d + (1 - odd) + extra)
+
+    big = steps - 1
+
+    def window(k, tail):
+        if tail:
+            size = HALF // TAIL
+            return pl.ds(HALF + (k - big) * size, size), rows - ROWS
+        return pl.ds((k // tiles) * HALF, HALF), pl.multiple_of(lax.rem(k, tiles) * ROWS, ROWS)
+
+    def each(body, head=True, tail=True):
+        def run(is_tail, k, _):
+            body(k, is_tail)
+            return 0
+        if head:
+            lax.fori_loop(0, big, functools.partial(run, False), 0)
+        if tail:
+            lax.fori_loop(big, big + TAIL, functools.partial(run, True), 0)
+
+    def own_chunk(k, tail):
+        part, r0 = window(k, tail)
+        return own.at[part, :, pl.ds(r0 + 8, ROWS), :]
+
+    def halo_chunk(slot, k, tail):
+        part, r0 = window(k, tail)
+        return halo.at[slot, part, :, pl.ds(r0, ROWS), :]
+
+    def via_chunk(k, tail):
+        part, r0 = window(k, tail)
+        return via.at[part, :, pl.ds(r0, ROWS), :]
 
     mine = 1 - odd
 
-    def to_partner(k):
+    def to_partner(k, tail):
         return pltpu.make_async_remote_copy(
-            own_chunk(k), halo_chunk(odd, k), send_p.at[k], recv_p.at[k],
+            own_chunk(k, tail), halo_chunk(odd, k, tail), send_p.at[k], recv_p.at[k],
             device_id={"dev": partner}, device_id_type=MESH)
 
-    def from_partner(k):
+    def relay(k, tail):
         return pltpu.make_async_remote_copy(
-            own_chunk(k), halo_chunk(mine, k), send_p.at[k], recv_p.at[k],
-            device_id={"dev": partner}, device_id_type=MESH)
-
-    def relay(k):
+            halo_chunk(mine, k, tail), halo_chunk(odd, k, tail), send_r.at[k], recv_r.at[k],
+            device_id=target_id, device_id_type=MESH)
+
+    def straight(k, tail):
         return pltpu.make_async_remote_copy(
-            halo_chunk(mine, k), halo_chunk(odd, k), send_r.at[k], recv_r.at[k],
-            device_id=target_id, device_id_type=MESH)
-
-    def straight(k):
+            own_chunk(k, tail), via_chunk(k, tail), send_d.at[k], recv_d.at[k],
+            device_id=hub_id, device_id_type=MESH)
+
+    def hand_on(k, tail):
         return pltpu.make_async_remote_copy(
-            own_chunk(k), halo_chunk(mine, k), send_d.at[k], recv_r.at[k],
-            device_id=nearby_id, device_id_type=MESH)
-
-    def first_sends(k, _):
-        to_partner(k).start()
+            via_chunk(k, tail), halo_chunk(mine, k, tail), send_r.at[k], recv_r.at[k],
+            device_id=hub_target, device_id_type=MESH)
+
+    def send(k, tail):
+        to_partner(k, tail).start()
+
+    def send_straight(k, tail):
+        straight(k, tail).start()
+
+    yields = (d == end) & (godd == 1)
+
+    def send_half(half):
+        def run(k, _):
+            send(k, False)
+            return 0
+
+        @pl.when(jnp.logical_not(yields))
+        def _():
+            lax.fori_loop(half * tiles, tiles if half == 0 else big, run, 0)
+
+    loads[0].wait()
+    send_half(0)
+
+    @pl.when((odd == 0) & (d >= 2))
+    def _():
+        pl.semaphore_signal(up, inc=1, device_id={"dev": d - 2}, device_id_type=MESH)
+
+    @pl.when((d == end) & (godd == 0))
+    def _():
+        pl.semaphore_signal(up, inc=1, device_id={**group(1), "dev": 1}, device_id_type=MESH)
+
+    @pl.when((d == end - 1) & (godd == 1))
+    def _():
+        pl.semaphore_signal(far, inc=1, device_id={**group(-1), "dev": 0}, device_id_type=MESH)
+
+    loads[1].wait()
+    send_half(1)
+
+    @pl.when(jnp.logical_not(yields))
+    def _():
+        each(send, head=False)
+
+    @pl.when(yields)
+    def _():
+        each(send_straight)
+
+    def reply(to, _):
+        pl.semaphore_signal(ready, inc=1, device_id={"dev": to}, device_id_type=MESH)
         return 0
 
-    loads[0].wait()
-    lax.fori_loop(0, tiles * SUB, first_sends, 0)
-    loads[1].wait()
-    lax.fori_loop(tiles * SUB, steps * SUB, first_sends, 0)
+    lax.fori_loop(0, d, reply, 0)
     loads[2].wait()
     loads[3].wait()
 
@@ -320,65 +403,105 @@
         lax.fori_loop(HALF // 4, F // 4, planes, 0)
         mixed(tile, HALF, F, False)
 
-    def relay_step(k, _):
-        from_partner(k).wait_recv()
+    asks = ((odd == 0) & (d < end - 1)) | ((d == 1) & (godd == 1))
+    hold_relay = jnp.where((d == 1) & (godd == 1), HOLD_R, 0)
+    hold_hub = jnp.where(d == 1, HOLD_V, 1)
+
+    def arrived(k, tail):
+        to_partner(k, tail).wait_recv()
+
+    def relayed(k, tail):
+        relay(k, tail).wait_recv()
+
+    def pass_on(k, tail):
+        straight(k, tail).wait_recv()
+        hand_on(k, tail).start()
+
+    def last_relay(k, tail):
+        arrived(k, tail)
 
         @pl.when(relays)
         def _():
-            relay(k).start()
+            relay(k, tail).start()
+
+    def step(part, _):
+        @pl.when(part < big)
+        def _():
+            arrived(part, False)
+
+        @pl.when(yields & (part == HOLD_P))
+        def _():
+            each(send)
+
+        @pl.when(direct & (d == 0) & (part == HOLD_D))
+        def _():
+            pl.semaphore_wait(far, 1)
+            each(send_straight)
+
+        r = part - hold_relay
+
+        @pl.when(relays & (r >= 0) & (r < big))
+        def _():
+            @pl.when(asks & (r == 0))
+            def _():
+                pl.semaphore_wait(up, 1)
+            relay(r, False).start()
+
+        @pl.when(r == big)
+        def _():
+            each(last_relay, head=False)
+
+        v = part - hold_hub
+
+        @pl.when(hub & (v >= 0) & (v < big))
+        def _():
+            pass_on(v, False)
+
+        @pl.when(hub & (v == big))
+        def _():
+            each(pass_on, head=False)
+
+        j = part - LAG
+
+        @pl.when((j >= 0) & (j < big))
+        def _():
+            relayed(j, False)
+
+        @pl.when(j == big)
+        def _():
+            each(relayed, head=False)
+
+        if WEYL:
+            @pl.when((j == 1) & (d < end))
+            def _():
+                pl.semaphore_wait(ready, end - d)
+
+            @pl.when((j >= 1) & (j <= tiles))
+            def _():
+                weyl_send(j - 1)
+
+        if COMPUTE:
+            @pl.when((j >= 0) & (j < tiles))
+            def _():
+                weyl_tile(j)
+                rhs_early(j)
+
+            @pl.when(j >= tiles)
+            def _():
+                rhs_late(j - tiles)
+        return 0
+
+    lax.fori_loop(0, steps + LAG, step, 0)
+
+    def sent_all(k, tail):
+        to_partner(k, tail).wait_send()
+        relay(k, tail).wait_send()
 
         @pl.when(direct)
         def _():
-            straight(k).start()
-        return 0
-
-    def relayed(k, _):
-        pltpu.make_async_remote_copy(
-            own_chunk(k), halo_chunk(odd, k), send_r.at[k], recv_r.at[k],
-            device_id={"dev": partner}, device_id_type=MESH).wait_recv()
-        return 0
-
-    def step(part, _):
-        @pl.when(part < steps)
-        def _():
-            lax.fori_loop(part * SUB, part * SUB + SUB, relay_step, 0)
-
-        j = part - LAG
-
-        @pl.when(j >= 0)
-        def _():
-            lax.fori_loop(j * SUB, j * SUB + SUB, relayed, 0)
-            if WEYL:
-                @pl.when((j >= 1) & (j <= tiles))
-                def _():
-                    weyl_send(j - 1)
-
-            if COMPUTE:
-                @pl.when(j < tiles)
-                def _():
-                    weyl_tile(j)
-                    rhs_early(j)
-
-                @pl.when(j >= tiles)
-                def _():
-                    rhs_late(j - tiles)
-        return 0
-
-    lax.fori_loop(0, steps + LAG, step, 0)
-
-    def finish(k, _):
-        to_partner(k).wait_send()
-
-        @pl.when(relays)
-        def _():
-            relay(k).wait_send()
-
-        @pl.when(direct)
-        def _():
-            straight(k).wait_send()
-        return 0
-
-    lax.fori_loop(0, steps * SUB, finish, 0)
+            straight(k, tail).wait_send()
+
+    each(sent_all)
     if WEYL:
         sent = wl.at[pl.ds(0, members - 1)]
         pltpu.make_async_copy(sent, sent, wsend).wait()
@@ -390,10 +513,11 @@
 def per_device(groups, members, fields, mix_matrix, laplace_matrix):
     depth, rows, width = fields.shape[1:]
     share = rows // members
-    chunks = 2 * (rows // ROWS) * SUB
+    chunks = 2 * (rows // ROWS) - 1 + TAIL
     arrays = [pltpu.with_memory_space_constraint(a, pltpu.HBM)
               for a in (fields, mix_matrix, laplace_matrix)]
     dma = pltpu.SemaphoreType.DMA
+    regular = pltpu.SemaphoreType.REGULAR
     return pl.pallas_call(
         functools.partial(kernel, groups, members),
         out_shape=(
@@ -409,6 +533,7 @@
         scratch_shapes=[
             pltpu.VMEM((F, depth, rows + 16, width), jnp.float32),
             pltpu.VMEM((2, F, depth, rows, width), jnp.float32),
+            pltpu.VMEM((F, depth, rows, width), jnp.float32),
             pltpu.VMEM((F, depth, ROWS, width), jnp.float32),
             pltpu.VMEM((F, F, 8, 128), jnp.float32),
             pltpu.VMEM((F, F, 8, 128), jnp.float32),
@@ -416,8 +541,8 @@
             pltpu.VMEM((F, F), jnp.float32),
             pltpu.VMEM((F, F), jnp.float32),
             pltpu.VMEM((2, F, F, 128), jnp.float32),
-            dma((6,)), dma((chunks,)), dma((chunks,)), dma((chunks,)), dma((chunks,)), dma((chunks,)),
-            dma, dma, dma,
+            dma((6,)), dma((chunks,)), dma((chunks,)), dma((chunks,)), dma((chunks,)), dma((chunks,)), dma((chunks,)),
+            dma, dma, dma, regular, regular, regular,
         ],
         compiler_params=pltpu.CompilerParams(
             collective_id=0, has_side_effects=True, vmem_limit_bytes=40 * 1024 * 1024

time: 91.1 us -> 87.7 us (0.963)
  the two profiles are of different devices: /device:TPU:1 before, /device:TPU:96 now
where the time goes in v3:
time: 87.7 us; the launch traced here: 86 us
  Pallas kernels  83 us (95%)
  local copies, waits for them, and re-layouts  2.37 us (3%)
    pallas_call x1, Pallas kernels, per_device(): pl.pallas_call(functools.partial(kernel, groups, members), out_shape=(jax...  83 us
    unnamed x2, local copies, waits for them, and re-layouts  2.37 us

profile of v3, /device:TPU:96, one launch (start us, length us, event | category | flops | bytes accessed | tf_op | source)
XLA Modules:
  0.0 86.0 jit_solution(17385542880556113994)
XLA Ops:
  0.6 83.0 %shard_map.50 = (f32[24,2,128,128]{3,2,1,0:T(8,128)S(1)}, f32[2,64,4,128]{3,2,1,0:T(4,128)S(1)}) custom-call(f32[24,2,128,128]{3,2,1,0:T(8,128)} %fields.1, f32[24,24]{1,0:T(8,128)} %mix_in.1, f32[24,24]{1,0:T(8,128)} %lap_in.1), custom_call_target="tpu_custom_call" | custom-call | tf_op jit(solution)/shard_map/pallas_call | solution.py:521
  83.6 1.7 %copy.7 = f32[24,2,128,128]{3,2,1,0:T(8,128)} copy(f32[24,2,128,128]{3,2,1,0:T(8,128)S(1)} %get-tuple-element.4) | data formatting | bytes 6291456
  85.3 0.7 copy.8

commit v4 on v3

--- a/solution.py
+++ b/solution.py
@@ -12,11 +12,12 @@
 HALF = 12
 ROWS = 8
 LAG = 8
-TAIL = 4
+PIECES = 2
 HOLD_P = 3
 HOLD_R = 2
 HOLD_D = 4
 HOLD_V = 5
+PARTS = 8
 BLOCK = 12
 COMPUTE = True
 WEYL = True
@@ -108,76 +109,90 @@
     extra = jnp.where(d == end, 1, jnp.where(d == end - 1, 1 + godd, jnp.where(d == 1, 1 - godd, 0)))
     pl.semaphore_wait(barrier, d + (1 - odd) + extra)
 
-    big = steps - 1
-
-    def window(k, tail):
-        if tail:
-            size = HALF // TAIL
-            return pl.ds(HALF + (k - big) * size, size), rows - ROWS
-        return pl.ds((k // tiles) * HALF, HALF), pl.multiple_of(lax.rem(k, tiles) * ROWS, ROWS)
-
-    def each(body, head=True, tail=True):
-        def run(is_tail, k, _):
-            body(k, is_tail)
+    size = HALF // PIECES
+    last = PIECES + steps - 2
+
+    def window(k, kind):
+        if kind == 0:
+            return pl.ds(k * size, size), 0
+        if kind == 2:
+            return pl.ds(HALF + (k - last) * size, size), rows - ROWS
+        part = k - (PIECES - 1)
+        return pl.ds((part // tiles) * HALF, HALF), pl.multiple_of(lax.rem(part, tiles) * ROWS, ROWS)
+
+    def run(kind, first, stop, body):
+        def once(k, _):
+            body(k, kind)
             return 0
-        if head:
-            lax.fori_loop(0, big, functools.partial(run, False), 0)
-        if tail:
-            lax.fori_loop(big, big + TAIL, functools.partial(run, True), 0)
-
-    def own_chunk(k, tail):
-        part, r0 = window(k, tail)
+        lax.fori_loop(first, stop, once, 0)
+
+    def each(body, low=0, high=steps):
+        if low == 0:
+            run(0, 0, PIECES, body)
+        run(1, max(low, 1) + PIECES - 1, min(high, steps - 1) + PIECES - 1, body)
+        if high == steps:
+            run(2, last, last + PIECES, body)
+
+    def at(part, body):
+        @pl.when(part == 0)
+        def _():
+            run(0, 0, PIECES, body)
+
+        @pl.when((part > 0) & (part < steps - 1))
+        def _():
+            body(part + PIECES - 1, 1)
+
+        @pl.when(part == steps - 1)
+        def _():
+            run(2, last, last + PIECES, body)
+
+    def own_chunk(k, kind):
+        part, r0 = window(k, kind)
         return own.at[part, :, pl.ds(r0 + 8, ROWS), :]
 
-    def halo_chunk(slot, k, tail):
-        part, r0 = window(k, tail)
+    def halo_chunk(slot, k, kind):
+        part, r0 = window(k, kind)
         return halo.at[slot, part, :, pl.ds(r0, ROWS), :]
 
-    def via_chunk(k, tail):
-        part, r0 = window(k, tail)
+    def via_chunk(k, kind):
+        part, r0 = window(k, kind)
         return via.at[part, :, pl.ds(r0, ROWS), :]
 
     mine = 1 - odd
 
-    def to_partner(k, tail):
+    def to_partner(k, kind):
         return pltpu.make_async_remote_copy(
-            own_chunk(k, tail), halo_chunk(odd, k, tail), send_p.at[k], recv_p.at[k],
+            own_chunk(k, kind), halo_chunk(odd, k, kind), send_p.at[k], recv_p.at[k],
             device_id={"dev": partner}, device_id_type=MESH)
 
-    def relay(k, tail):
+    def relay(k, kind):
         return pltpu.make_async_remote_copy(
-            halo_chunk(mine, k, tail), halo_chunk(odd, k, tail), send_r.at[k], recv_r.at[k],
+            halo_chunk(mine, k, kind), halo_chunk(odd, k, kind), send_r.at[k], recv_r.at[k],
             device_id=target_id, device_id_type=MESH)
 
-    def straight(k, tail):
+    def straight(k, kind):
         return pltpu.make_async_remote_copy(
-            own_chunk(k, tail), via_chunk(k, tail), send_d.at[k], recv_d.at[k],
+            own_chunk(k, kind), via_chunk(k, kind), send_d.at[k], recv_d.at[k],
             device_id=hub_id, device_id_type=MESH)
 
-    def hand_on(k, tail):
+    def hand_on(k, kind):
         return pltpu.make_async_remote_copy(
-            via_chunk(k, tail), halo_chunk(mine, k, tail), send_r.at[k], recv_r.at[k],
+            via_chunk(k, kind), halo_chunk(mine, k, kind), send_r.at[k], recv_r.at[k],
             device_id=hub_target, device_id_type=MESH)
 
-    def send(k, tail):
-        to_partner(k, tail).start()
-
-    def send_straight(k, tail):
-        straight(k, tail).start()
+    def send(k, kind):
+        to_partner(k, kind).start()
+
+    def send_straight(k, kind):
+        straight(k, kind).start()
 
     yields = (d == end) & (godd == 1)
 
-    def send_half(half):
-        def run(k, _):
-            send(k, False)
-            return 0
-
-        @pl.when(jnp.logical_not(yields))
-        def _():
-            lax.fori_loop(half * tiles, tiles if half == 0 else big, run, 0)
-
     loads[0].wait()
-    send_half(0)
+
+    @pl.when(jnp.logical_not(yields))
+    def _():
+        each(send, 0, tiles)
 
     @pl.when((odd == 0) & (d >= 2))
     def _():
@@ -192,11 +207,10 @@
         pl.semaphore_signal(far, inc=1, device_id={**group(-1), "dev": 0}, device_id_type=MESH)
 
     loads[1].wait()
-    send_half(1)
 
     @pl.when(jnp.logical_not(yields))
     def _():
-        each(send, head=False)
+        each(send, tiles, steps)
 
     @pl.when(yields)
     def _():
@@ -214,14 +228,14 @@
     loads[5].wait()
     if COMPUTE:
         lap_all = lapw[...]
-        for at, table in enumerate((mix[...] - 7.5 * lap_all, lap_all * (1.0 / 12.0))):
+        for slot, table in enumerate((mix[...] - 7.5 * lap_all, lap_all * (1.0 / 12.0))):
             for h in range(F):
-                wrow[at, h] = jnp.broadcast_to(table[:, h:h + 1], (F, 128))
+                wrow[slot, h] = jnp.broadcast_to(table[:, h:h + 1], (F, 128))
 
         def spread(h, _):
-            for at, into in enumerate((w1, w2)):
+            for slot, into in enumerate((w1, w2)):
                 for c in range(F):
-                    into[h, c] = jnp.broadcast_to(wrow[at, h, c:c + 1, :], (8, 128))
+                    into[h, c] = jnp.broadcast_to(wrow[slot, h, c:c + 1, :], (8, 128))
             return 0
 
         lax.fori_loop(0, F, spread, 0)
@@ -230,14 +244,14 @@
     line = lax.broadcasted_iota(jnp.int32, (ROWS, width), 0).astype(jnp.float32)
 
     def near(h, r0, p, halos=True):
-        def at(off):
+        def along(off):
             return own[h, p, pl.ds(r0 + 8 + off, ROWS), :]
         mid = pl.ds(pl.multiple_of(r0 + 8, 8), ROWS)
         here = own[h, p, mid, :]
         rows_at = pl.ds(pl.multiple_of(r0, 8), ROWS)
         xs = [pltpu.roll(here, 2, 1), pltpu.roll(here, 1, 1),
               pltpu.roll(here, width - 1, 1), pltpu.roll(here, width - 2, 1)]
-        ys = [at(-2), at(-1), at(1), at(2)]
+        ys = [along(-2), along(-1), along(1), along(2)]
         other = own[h, 1 - p, mid, :]
         if not halos:
             return here, xs, ys, other
@@ -285,10 +299,10 @@
 
             real = None
             imag = None
-            for at, (i, j) in enumerate(pairs):
-                here, xs, ys, zs = near(at, r0, p)
+            for comp, (i, j) in enumerate(pairs):
+                here, xs, ys, zs = near(comp, r0, p)
                 lap = lap_sum(xs, ys, zs) - 90.0 * here
-                elec = lap * (-0.5 / 12.0) - trace * curv[at]
+                elec = lap * (-0.5 / 12.0) - trace * curv[comp]
                 for m in range(3):
                     elec = elec + curv[table[i][m]] * curv[table[m][j]]
                 if i == j:
@@ -404,30 +418,53 @@
         mixed(tile, HALF, F, False)
 
     asks = ((odd == 0) & (d < end - 1)) | ((d == 1) & (godd == 1))
-    hold_relay = jnp.where((d == 1) & (godd == 1), HOLD_R, 0)
+    held = (d == 1) & (godd == 1)
     hold_hub = jnp.where(d == 1, HOLD_V, 1)
 
-    def arrived(k, tail):
-        to_partner(k, tail).wait_recv()
-
-    def relayed(k, tail):
-        relay(k, tail).wait_recv()
-
-    def pass_on(k, tail):
-        straight(k, tail).wait_recv()
-        hand_on(k, tail).start()
-
-    def last_relay(k, tail):
-        arrived(k, tail)
-
-        @pl.when(relays)
-        def _():
-            relay(k, tail).start()
+    def ask():
+        @pl.when(asks)
+        def _():
+            pl.semaphore_wait(up, 1)
+
+    def arrived(k, kind):
+        to_partner(k, kind).wait_recv()
+
+        @pl.when(relays & jnp.logical_not(held))
+        def _():
+            relay(k, kind).start()
+
+    def late_relay(k, kind):
+        relay(k, kind).start()
+
+    def pass_on(k, kind):
+        straight(k, kind).wait_recv()
+        hand_on(k, kind).start()
+
+    def done(k, kind):
+        relay(k, kind).wait_recv()
+        to_partner(k, kind).wait_send()
+        relay(k, kind).wait_send()
+
+        @pl.when(direct)
+        def _():
+            straight(k, kind).wait_send()
+
+    def passed(part):
+        return jnp.minimum(jnp.minimum(jnp.maximum(2 * (part - hold_hub), 0), part), steps)
 
     def step(part, _):
-        @pl.when(part < big)
-        def _():
-            arrived(part, False)
+        @pl.when((part == 0) & jnp.logical_not(held))
+        def _():
+            ask()
+
+        at(part, arrived)
+
+        @pl.when(held)
+        def _():
+            @pl.when(part == HOLD_R)
+            def _():
+                ask()
+            at(part - HOLD_R, late_relay)
 
         @pl.when(yields & (part == HOLD_P))
         def _():
@@ -438,44 +475,21 @@
             pl.semaphore_wait(far, 1)
             each(send_straight)
 
-        r = part - hold_relay
-
-        @pl.when(relays & (r >= 0) & (r < big))
-        def _():
-            @pl.when(asks & (r == 0))
-            def _():
-                pl.semaphore_wait(up, 1)
-            relay(r, False).start()
-
-        @pl.when(r == big)
-        def _():
-            each(last_relay, head=False)
-
-        v = part - hold_hub
-
-        @pl.when(hub & (v >= 0) & (v < big))
-        def _():
-            pass_on(v, False)
-
-        @pl.when(hub & (v == big))
-        def _():
-            each(pass_on, head=False)
+        @pl.when(hub)
+        def _():
+            def catch_up(v, _):
+                at(v, pass_on)
+                return 0
+            lax.fori_loop(passed(part), passed(part + 1), catch_up, 0)
 
         j = part - LAG
-
-        @pl.when((j >= 0) & (j < big))
-        def _():
-            relayed(j, False)
-
-        @pl.when(j == big)
-        def _():
-            each(relayed, head=False)
+        at(j, done)
+
+        @pl.when((j == 1) & (d < end))
+        def _():
+            pl.semaphore_wait(ready, end - d)
 
         if WEYL:
-            @pl.when((j == 1) & (d < end))
-            def _():
-                pl.semaphore_wait(ready, end - d)
-
             @pl.when((j >= 1) & (j <= tiles))
             def _():
                 weyl_send(j - 1)
@@ -493,15 +507,6 @@
 
     lax.fori_loop(0, steps + LAG, step, 0)
 
-    def sent_all(k, tail):
-        to_partner(k, tail).wait_send()
-        relay(k, tail).wait_send()
-
-        @pl.when(direct)
-        def _():
-            straight(k, tail).wait_send()
-
-    each(sent_all)
     if WEYL:
         sent = wl.at[pl.ds(0, members - 1)]
         pltpu.make_async_copy(sent, sent, wsend).wait()
@@ -510,20 +515,30 @@
         pltpu.make_async_copy(wl.at[0], weyl.at[:, pl.ds(0, depth)], wlocal).wait()
 
 
+def put_out(rhs_in, weyl_in, rhs, weyl, sem):
+    each = F // PARTS
+    copies = [pltpu.make_async_copy(weyl_in, weyl, sem.at[PARTS])]
+    for k in range(PARTS):
+        part = pl.ds(k * each, each)
+        copies.append(pltpu.make_async_copy(rhs_in.at[part], rhs.at[part], sem.at[k]))
+    for copy in copies:
+        copy.start()
+    for copy in copies:
+        copy.wait()
+
+
 def per_device(groups, members, fields, mix_matrix, laplace_matrix):
     depth, rows, width = fields.shape[1:]
     share = rows // members
-    chunks = 2 * (rows // ROWS) - 1 + TAIL
+    chunks = 2 * (rows // ROWS) - 2 + 2 * PIECES
     arrays = [pltpu.with_memory_space_constraint(a, pltpu.HBM)
               for a in (fields, mix_matrix, laplace_matrix)]
     dma = pltpu.SemaphoreType.DMA
     regular = pltpu.SemaphoreType.REGULAR
-    return pl.pallas_call(
+    shapes = (fields.shape, (2, depth * members, share, width))
+    results = pl.pallas_call(
         functools.partial(kernel, groups, members),
-        out_shape=(
-            jax.ShapeDtypeStruct(fields.shape, jnp.float32),
-            jax.ShapeDtypeStruct((2, depth * members, share, width), jnp.float32),
-        ),
+        out_shape=tuple(pltpu.VMEM(shape, jnp.float32) for shape in shapes),
         in_specs=[
             pl.BlockSpec(memory_space=pltpu.HBM),
             pl.BlockSpec(memory_space=pltpu.HBM),
@@ -548,6 +563,14 @@
             collective_id=0, has_side_effects=True, vmem_limit_bytes=40 * 1024 * 1024
         ),
     )(*arrays)
+    return pl.pallas_call(
+        put_out,
+        out_shape=tuple(pltpu.HBM(shape, jnp.float32) for shape in shapes),
+        in_specs=[pl.BlockSpec(memory_space=pltpu.VMEM)] * 2,
+        out_specs=(pl.BlockSpec(memory_space=pltpu.HBM),) * 2,
+        scratch_shapes=[pltpu.SemaphoreType.DMA((PARTS + 1,))],
+        compiler_params=pltpu.CompilerParams(vmem_limit_bytes=1024 * 1024),
+    )(*results)
 
 
 def solution(mesh):

time: 87.7 us -> 85.4 us (0.974); the launches traced: 86 us -> 85.1 us
  local copies, waits for them, and re-layouts: 2.37 us -> 0 us
  Pallas kernels: 83 us -> 84.4 us
    unnamed x2 -> x0, local copies, waits for them, and re-layouts: 2.37 us -> none
    pallas_call x1 -> x2, Pallas kernels: 83 us -> 84.4 us  [the longest x1 82.6 us: per_device(): pl.pallas_call(functools.partial(kernel, groups, members), out_shape=tupl...]
where the time goes in v4:
time: 85.4 us; the launch traced here: 85.1 us
  Pallas kernels  84.4 us (99%)
    pallas_call x1, Pallas kernels, per_device(): pl.pallas_call(functools.partial(kernel, groups, members), out_shape=tupl...  82.6 us
    pallas_call x1, Pallas kernels, per_device(): pl.pallas_call(put_out, out_shape=tuple((pltpu.HBM(shape, jnp.float32) fo...  1.82 us

profile of v4, /device:TPU:96, one launch (start us, length us, event | category | flops | bytes accessed | tf_op | source)
XLA Modules:
  0.0 85.1 jit_solution(5658725898227423042)
XLA Ops:
  0.6 82.6 %shard_map.50 = (f32[24,2,128,128]{3,2,1,0:T(8,128)S(1)}, f32[2,64,4,128]{3,2,1,0:T(4,128)S(1)}) custom-call(f32[24,2,128,128]{3,2,1,0:T(8,128)} %fields.1, f32[24,24]{1,0:T(8,128)} %mix_in.1, f32[24,24]{1,0:T(8,128)} %lap_in.1), custom_call_target="tpu_custom_call" | custom-call | tf_op jit(solution)/shard_map/pallas_call | solution.py:539
  83.3 1.8 %shard_map.51 = (f32[24,2,128,128]{3,2,1,0:T(8,128)}, f32[2,64,4,128]{3,2,1,0:T(4,128)}) custom-call(f32[24,2,128,128]{3,2,1,0:T(8,128)S(1)} %get-tuple-element.4.rhs_in, f32[2,64,4,128]{3,2,1,0:T(4,128)S(1)} %get-tuple-element.5.weyl_in), custom_call_target="tpu_custom_call" | custom-call | tf_op jit(solution)/shard_map/pallas_call | solution.py:566

commit v5 on v4

--- a/solution.py
+++ b/solution.py
@@ -13,11 +13,15 @@
 ROWS = 8
 LAG = 8
 PIECES = 2
-HOLD_P = 3
+HOLD_P = 1
 HOLD_R = 2
 HOLD_D = 4
 HOLD_V = 5
 PARTS = 8
+AHEAD = 20
+TURN_END = 24
+EVERY = 8
+HOLD_F = 3
 BLOCK = 12
 COMPUTE = True
 WEYL = True
@@ -29,7 +33,7 @@
 
 def kernel(groups, members, fields, mix_in, lap_in, rhs, weyl, own, halo, via, tsum, w1, w2, wl,
            mix, lapw, wrow, load_sem, send_p, recv_p, send_r, recv_r, send_d, recv_d, wsend, wrecv, wlocal,
-           up, far, ready):
+           up, far, ready, send_f, over):
     depth = fields.shape[1]
     rows = fields.shape[2]
     width = fields.shape[3]
@@ -106,7 +110,22 @@
     def _():
         hello({**group(2), "dev": end - 1})
 
-    extra = jnp.where(d == end, 1, jnp.where(d == end - 1, 1 + godd, jnp.where(d == 1, 1 - godd, 0)))
+    wide = ((odd == 0) & (d <= end - 3)) | ((odd == 1) & (d >= 3))
+
+    @pl.when((odd == 0) & (d <= end - 3))
+    def _():
+        hello({**group(2), "dev": d + 3})
+
+    @pl.when((odd == 0) & (d >= 2))
+    def _():
+        hello({**group(2), "dev": d + 1})
+
+    @pl.when((odd == 1) & (d < end))
+    def _():
+        hello({**group(2), "dev": d - 1})
+
+    wider = jnp.where(wide, 1 + odd, 0)
+    extra = wider + jnp.where(d == end, 1, jnp.where(d == end - 1, 1 + godd, jnp.where(d == 1, 1 - godd, 0)))
     pl.semaphore_wait(barrier, d + (1 - odd) + extra)
 
     size = HALF // PIECES
@@ -180,6 +199,19 @@
             via_chunk(k, kind), halo_chunk(mine, k, kind), send_r.at[k], recv_r.at[k],
             device_id=hub_target, device_id_type=MESH)
 
+    def detour(k, kind):
+        return pltpu.make_async_remote_copy(
+            halo_chunk(mine, k, kind), via_chunk(k, kind), send_r.at[k], recv_d.at[k],
+            device_id={**group(2), "dev": d + 3 - 6 * odd}, device_id_type=MESH)
+
+    def hand_back(k, kind):
+        return pltpu.make_async_remote_copy(
+            via_chunk(k, kind), halo_chunk(mine, k, kind), send_f.at[k], recv_r.at[k],
+            device_id={**group(2), "dev": partner}, device_id_type=MESH)
+
+    def turn(part):
+        return wide & (part > 0) & (part < TURN_END) & (lax.rem(part, EVERY) == EVERY - 1)
+
     def send(k, kind):
         to_partner(k, kind).start()
 
@@ -192,12 +224,16 @@
 
     @pl.when(jnp.logical_not(yields))
     def _():
-        each(send, 0, tiles)
+        each(send, 0, min(AHEAD, tiles))
 
     @pl.when((odd == 0) & (d >= 2))
     def _():
         pl.semaphore_signal(up, inc=1, device_id={"dev": d - 2}, device_id_type=MESH)
 
+    @pl.when((odd == 1) & (d >= 3))
+    def _():
+        pl.semaphore_signal(over, inc=1, device_id={**group(2), "dev": d - 3}, device_id_type=MESH)
+
     @pl.when((d == end) & (godd == 0))
     def _():
         pl.semaphore_signal(up, inc=1, device_id={**group(1), "dev": 1}, device_id_type=MESH)
@@ -208,9 +244,10 @@
 
     loads[1].wait()
 
-    @pl.when(jnp.logical_not(yields))
-    def _():
-        each(send, tiles, steps)
+    if AHEAD > tiles:
+        @pl.when(jnp.logical_not(yields))
+        def _():
+            each(send, tiles, AHEAD)
 
     @pl.when(yields)
     def _():
@@ -428,10 +465,20 @@
 
     def arrived(k, kind):
         to_partner(k, kind).wait_recv()
-
-        @pl.when(relays & jnp.logical_not(held))
-        def _():
-            relay(k, kind).start()
+        if kind == 1:
+            astray = turn(k - (PIECES - 1))
+
+            @pl.when(astray)
+            def _():
+                detour(k, kind).start()
+
+            @pl.when(relays & jnp.logical_not(held | astray))
+            def _():
+                relay(k, kind).start()
+        else:
+            @pl.when(relays & jnp.logical_not(held))
+            def _():
+                relay(k, kind).start()
 
     def late_relay(k, kind):
         relay(k, kind).start()
@@ -444,6 +491,10 @@
         relay(k, kind).wait_recv()
         to_partner(k, kind).wait_send()
         relay(k, kind).wait_send()
+        if kind == 1:
+            @pl.when(turn(k - (PIECES - 1)))
+            def _():
+                hand_back(k, kind).wait_send()
 
         @pl.when(direct)
         def _():
@@ -457,7 +508,17 @@
         def _():
             ask()
 
+        @pl.when((part == EVERY - 1) & wide & (odd == 0))
+        def _():
+            pl.semaphore_wait(over, 1)
+
         at(part, arrived)
+
+        @pl.when(turn(part - HOLD_F))
+        def _():
+            k = part - HOLD_F + PIECES - 1
+            straight(k, 1).wait_recv()
+            hand_back(k, 1).start()
 
         @pl.when(held)
         def _():
@@ -468,7 +529,11 @@
 
         @pl.when(yields & (part == HOLD_P))
         def _():
-            each(send)
+            each(send, 0, AHEAD + HOLD_P)
+
+        @pl.when(jnp.logical_not(yields & (part < HOLD_P)))
+        def _():
+            at(part + AHEAD, send)
 
         @pl.when(direct & (d == 0) & (part == HOLD_D))
         def _():
@@ -558,6 +623,7 @@
             pltpu.VMEM((2, F, F, 128), jnp.float32),
             dma((6,)), dma((chunks,)), dma((chunks,)), dma((chunks,)), dma((chunks,)), dma((chunks,)), dma((chunks,)),
             dma, dma, dma, regular, regular, regular,
+            dma((chunks,)), regular,
         ],
         compiler_params=pltpu.CompilerParams(
             collective_id=0, has_side_effects=True, vmem_limit_bytes=40 * 1024 * 1024

time: 85.4 us -> 83.9 us (0.982)
  Pallas kernels: 84.4 us -> 83.2 us
    pallas_call x1, Pallas kernels: 82.6 us -> 81.3 us  [per_device(): pl.pallas_call(functools.partial(kernel, groups, members), out_shape=tupl...]
where the time goes in v5:
time: 83.9 us; the launch traced here: 83.8 us
  Pallas kernels  83.2 us (99%)
    pallas_call x1, Pallas kernels, per_device(): pl.pallas_call(functools.partial(kernel, groups, members), out_shape=tupl...  81.3 us
    pallas_call x1, Pallas kernels, per_device(): pl.pallas_call(put_out, out_shape=tuple((pltpu.HBM(shape, jnp.float32) fo...  1.82 us

profile of v5, /device:TPU:96, one launch (start us, length us, event | category | flops | bytes accessed | tf_op | source)
XLA Modules:
  0.0 83.8 jit_solution(7466761915862217832)
XLA Ops:
  0.6 81.3 %shard_map.50 = (f32[24,2,128,128]{3,2,1,0:T(8,128)S(1)}, f32[2,64,4,128]{3,2,1,0:T(4,128)S(1)}) custom-call(f32[24,2,128,128]{3,2,1,0:T(8,128)} %fields.1, f32[24,24]{1,0:T(8,128)} %mix_in.1, f32[24,24]{1,0:T(8,128)} %lap_in.1), custom_call_target="tpu_custom_call" | custom-call | tf_op jit(solution)/shard_map/pallas_call | solution.py:604
  82.0 1.8 %shard_map.51 = (f32[24,2,128,128]{3,2,1,0:T(8,128)}, f32[2,64,4,128]{3,2,1,0:T(4,128)}) custom-call(f32[24,2,128,128]{3,2,1,0:T(8,128)S(1)} %get-tuple-element.4.rhs_in, f32[2,64,4,128]{3,2,1,0:T(4,128)S(1)} %get-tuple-element.5.weyl_in), custom_call_target="tpu_custom_call" | custom-call | tf_op jit(solution)/shard_map/pallas_call | solution.py:632

commit v6 on v5

--- a/solution.py
+++ b/solution.py
@@ -12,7 +12,7 @@
 HALF = 12
 ROWS = 8
 LAG = 8
-PIECES = 2
+PIECES = 1
 HOLD_P = 1
 HOLD_R = 2
 HOLD_D = 4
@@ -60,11 +60,15 @@
     hub_id = {"grp": lax.rem(g + 1 - 2 * godd + groups, groups), "dev": jnp.where(d == 0, end - 1, 1)}
     hub_target = {**group(2), "dev": jnp.where(d == 1, 0, end)}
 
-    loads = []
-    for half in range(2):
-        part = pl.ds(half * HALF, HALF)
-        loads.append(pltpu.make_async_copy(
-            fields.at[part], own.at[part, :, pl.ds(8, rows), :], load_sem.at[half]))
+    low, high = pl.ds(0, HALF), pl.ds(HALF, HALF)
+    opening = pltpu.make_async_copy(
+        fields.at[low, :, pl.ds(0, ROWS), :], own.at[low, :, pl.ds(8, ROWS), :], load_sem.at[6])
+    opening.start()
+    loads = [pltpu.make_async_copy(
+        fields.at[low, :, pl.ds(ROWS, rows - ROWS), :],
+        own.at[low, :, pl.ds(8 + ROWS, rows - ROWS), :], load_sem.at[0])]
+    loads.append(pltpu.make_async_copy(
+        fields.at[high], own.at[high, :, pl.ds(8, rows), :], load_sem.at[1]))
     loads.append(pltpu.make_async_copy(
         fields.at[:, :, pl.ds(rows - 8, 8), :], own.at[:, :, pl.ds(0, 8), :], load_sem.at[2]))
     loads.append(pltpu.make_async_copy(
@@ -220,11 +224,17 @@
 
     yields = (d == end) & (godd == 1)
 
+    opening.wait()
+
+    @pl.when(jnp.logical_not(yields))
+    def _():
+        each(send, 0, 1)
+
     loads[0].wait()
 
     @pl.when(jnp.logical_not(yields))
     def _():
-        each(send, 0, min(AHEAD, tiles))
+        each(send, 1, min(AHEAD, tiles))
 
     @pl.when((odd == 0) & (d >= 2))
     def _():
@@ -621,7 +631,7 @@
             pltpu.VMEM((F, F), jnp.float32),
             pltpu.VMEM((F, F), jnp.float32),
             pltpu.VMEM((2, F, F, 128), jnp.float32),
-            dma((6,)), dma((chunks,)), dma((chunks,)), dma((chunks,)), dma((chunks,)), dma((chunks,)), dma((chunks,)),
+            dma((7,)), dma((chunks,)), dma((chunks,)), dma((chunks,)), dma((chunks,)), dma((chunks,)), dma((chunks,)),
             dma, dma, dma, regular, regular, regular,
             dma((chunks,)), regular,
         ],

time: 83.9 us -> 83.8 us (level)
  no operation moved by 1% of the time
where the time goes in v6:
time: 83.8 us; the launch traced here: 83.7 us
  Pallas kernels  83 us (99%)
    pallas_call x1, Pallas kernels, per_device(): pl.pallas_call(functools.partial(kernel, groups, members), out_shape=tupl...  81.2 us
    pallas_call x1, Pallas kernels, per_device(): pl.pallas_call(put_out, out_shape=tuple((pltpu.HBM(shape, jnp.float32) fo...  1.82 us

profile of v6, /device:TPU:96, one launch (start us, length us, event | category | flops | bytes accessed | tf_op | source)
XLA Modules:
  0.0 83.7 jit_solution(6345833676686475221)
XLA Ops:
  0.6 81.2 %shard_map.50 = (f32[24,2,128,128]{3,2,1,0:T(8,128)S(1)}, f32[2,64,4,128]{3,2,1,0:T(4,128)S(1)}) custom-call(f32[24,2,128,128]{3,2,1,0:T(8,128)} %fields.1, f32[24,24]{1,0:T(8,128)} %mix_in.1, f32[24,24]{1,0:T(8,128)} %lap_in.1), custom_call_target="tpu_custom_call" | custom-call | tf_op jit(solution)/shard_map/pallas_call | solution.py:614
  81.9 1.8 %shard_map.51 = (f32[24,2,128,128]{3,2,1,0:T(8,128)}, f32[2,64,4,128]{3,2,1,0:T(4,128)}) custom-call(f32[24,2,128,128]{3,2,1,0:T(8,128)S(1)} %get-tuple-element.4.rhs_in, f32[2,64,4,128]{3,2,1,0:T(4,128)S(1)} %get-tuple-element.5.weyl_in), custom_call_target="tpu_custom_call" | custom-call | tf_op jit(solution)/shard_map/pallas_call | solution.py:642

commit v7 on v6

--- a/solution.py
+++ b/solution.py
@@ -17,7 +17,7 @@
 HOLD_R = 2
 HOLD_D = 4
 HOLD_V = 5
-PARTS = 8
+PARTS = 4
 AHEAD = 20
 TURN_END = 24
 EVERY = 8

time: 83.8 us -> 83.8 us (level)
  no operation moved by 1% of the time
where the time goes in v7:
time: 83.8 us; the launch traced here: 83.6 us
  Pallas kernels  83 us (99%)
    pallas_call x1, Pallas kernels, per_device(): pl.pallas_call(functools.partial(kernel, groups, members), out_shape=tupl...  81.2 us
    pallas_call x1, Pallas kernels, per_device(): pl.pallas_call(put_out, out_shape=tuple((pltpu.HBM(shape, jnp.float32) fo...  1.79 us

profile of v7, /device:TPU:96, one launch (start us, length us, event | category | flops | bytes accessed | tf_op | source)
XLA Modules:
  0.0 83.6 jit_solution(10045234999041908582)
XLA Ops:
  0.6 81.2 %shard_map.50 = (f32[24,2,128,128]{3,2,1,0:T(8,128)S(1)}, f32[2,64,4,128]{3,2,1,0:T(4,128)S(1)}) custom-call(f32[24,2,128,128]{3,2,1,0:T(8,128)} %fields.1, f32[24,24]{1,0:T(8,128)} %mix_in.1, f32[24,24]{1,0:T(8,128)} %lap_in.1), custom_call_target="tpu_custom_call" | custom-call | tf_op jit(solution)/shard_map/pallas_call | solution.py:614
  81.9 1.8 %shard_map.51 = (f32[24,2,128,128]{3,2,1,0:T(8,128)}, f32[2,64,4,128]{3,2,1,0:T(4,128)}) custom-call(f32[24,2,128,128]{3,2,1,0:T(8,128)S(1)} %get-tuple-element.4.rhs_in, f32[2,64,4,128]{3,2,1,0:T(4,128)S(1)} %get-tuple-element.5.weyl_in), custom_call_target="tpu_custom_call" | custom-call | tf_op jit(solution)/shard_map/pallas_call | solution.py:642
